TPU v7x, 1024 devices: a whole 4x8x16 slice. The times are simulated.
1024 devices in a mesh: row: 32 (over z_hi, x, core), col: 32 (over z_lo, y).
Axes of the slice: x: 4, y: 8, z: 16 (z_hi: 4, z_lo: 4; z = z_hi * 4 + z_lo), core: 2. Of those that a mesh axis runs over, the one named last changes fastest.
Arguments:
- pressure_rhs: bfloat16 [384, 256, 384], P('col', 'row'), may hold values from -10 to 10, as said below
- scalar_source: bfloat16 [384, 256, 384], P('col', 'row'), may hold values from -10 to 10, as said below
- forward_y: bfloat16 [256, 256], replicated, may hold values from -0.375 to 0.375
- back_y: bfloat16 [256, 256], replicated, may hold values from -0.375 to 0.375
- wall_rates: float32 [256], replicated, may hold values from 0.05 to 4
Outputs:
- pressure: bfloat16 [384, 256, 384], P('col', 'row')
- scalar: bfloat16 [384, 256, 384], P('col', 'row')
Inputs may be any that keep to these rules, and one draw needn't show every extreme that they name: `pressure_rhs`: a real field of order one. `scalar_source`: a real field of order one.
All inputs are finite; a program needn't handle non-finite values.
Results may differ from a plain program's by a relative error of at most 0.012.
Values may be sent and summed in bfloat16 or wider, within the bound.
No kernel may reach another device: no remote copies, remote signals or barrier semaphores. Data moves between devices by JAX's collectives and lax.ppermute only.
A program may use at most 32 MiB of HBM per device.

v0:
```python
import math

import jax
import jax.numpy as jnp
import numpy as np
from jax import lax
from jax.experimental import pallas as pl
from jax.experimental.pallas import tpu as pltpu
from jax.sharding import PartitionSpec as P

NX = 384
NY = 256
NZ = 384
KEEP = 256
DIFFUSION = 0.5
G = 32
ZL = NZ // G
YL = NY // G
PER = NX // 2 // G
ITEMS = 2 * PER
WAVES = KEEP // G
LANES = 128
BF = jnp.bfloat16
F32 = jnp.float32

KEPT = np.array([t for t in range(NZ // G) if G * t < KEEP // 2 or G * t >= NZ - KEEP // 2])


def pairs(part_out, part_in, cos, sin, sign):
    if part_out == part_in:
        return cos
    return sign * sin if part_out == 1 else -sign * sin


def items():
    for i in range(ITEMS):
        yield i // 8, i % 8, i // PER, i % PER


def x_tables():
    fwd = np.zeros((2, G, 8, NX))
    back = np.zeros((2, G, 8, NX))
    x = np.arange(NX)
    factor = math.sqrt(2.0 / NX)
    for h, i, p, k in items():
        m = np.arange(G)[:, None] * PER + k
        angle = 2.0 * math.pi * (m * x[None, :] % NX) / NX
        value = factor * (np.cos(angle) if p == 0 else -np.sin(angle))
        fwd[h, :, i] = value
        back[h, :, i] = np.where(m == 0, 0.5, 1.0) * value
    return fwd.reshape(-1, NX), back.reshape(-1, NX)


def z_outer(sign):
    out = np.zeros((2, G, 8, 2, G, 8))
    angle = 2.0 * math.pi * (np.outer(np.arange(G), np.arange(G)) % G) / G
    cos, sin = np.cos(angle) / math.sqrt(G), np.sin(angle) / math.sqrt(G)
    for h, i, p, k in items():
        for q in range(2):
            out[q, :, k, h, :, i] = pairs(q, p, cos, sin, sign)
    return out.reshape(2 * G * 8, 2 * G * 8)


def z_outer_back():
    out = np.zeros((2, G, 8, 2, G, 8))
    angle = 2.0 * math.pi * (np.outer(np.arange(G), np.arange(G)) % G) / G
    cos, sin = np.cos(angle) / math.sqrt(G), np.sin(angle) / math.sqrt(G)
    for h, i, p, k in items():
        for q in range(2):
            out[h, :, i, q, :, k] = pairs(p, q, cos, sin, 1)
    return out.reshape(2 * G * 8, 2 * G * 8)


def z_inner(sign):
    out = np.zeros((2, WAVES, YL, 2, LANES))
    angle = 2.0 * math.pi * (np.outer(KEPT, np.arange(ZL)) % ZL) / ZL
    cos, sin = np.cos(angle) / math.sqrt(ZL), np.sin(angle) / math.sqrt(ZL)
    for a in range(2):
        for b in range(2):
            w = pairs(a, b, cos, sin, -1) if sign < 0 else pairs(b, a, cos, sin, 1)
            for y in range(YL):
                out[a, :, y, b, y : ZL * YL : YL] = w
    return out.reshape(2 * WAVES * YL, 2 * LANES)


def twiddles():
    angle = 2.0 * math.pi * np.outer(np.arange(G), np.arange(ZL)) / NZ
    angle = np.repeat(np.repeat(angle, 8, axis=0), YL, axis=1)
    pad = LANES - ZL * YL
    return np.pad(np.cos(angle), ((0, 0), (0, pad))), np.pad(np.sin(angle), ((0, 0), (0, pad)))


def dot(a, b, ca=1, cb=0):
    return lax.dot_general(a, b, (((ca,), (cb,)), ((), ())), preferred_element_type=F32)


def pack(g, roll):
    n = G * 8
    mid = g[n:, :LANES] + roll(g[n:, LANES:], 4, 0)
    tiles = [v.reshape(G, 8, LANES) for v in (g[:n, :LANES], mid, g[:n, LANES:])]
    return jnp.concatenate(tiles, axis=1).reshape(G * 24, LANES).astype(BF)


def unpack(x, roll):
    n = G * 8
    x = x.astype(F32).reshape(G, 24, LANES)
    first, mid, last = (x[:, 8 * j : 8 * j + 8].reshape(n, LANES) for j in range(3))
    return (
        jnp.concatenate((first, mid), axis=0).astype(BF),
        jnp.concatenate((last, roll(mid, n - 4, 0)), axis=0).astype(BF),
    )


def swap_blocks(rows, roll):
    lane = lax.broadcasted_iota(jnp.int32, (8, LANES), 1) // 8
    x = list(rows)
    for d in (8, 4, 2, 1):
        high = (lane & d) != 0
        for i in range(16):
            if not i & d:
                a, b = x[i], x[i + d]
                x[i] = jnp.where(high, roll(b, 8 * d, 1), a)
                x[i + d] = jnp.where(high, b, roll(a, LANES - 8 * d, 1))
    return x


def stage1(p, s, table, roll):
    zero = jnp.zeros((LANES - ZL * YL, NX), BF)
    both = jnp.concatenate((p, zero, s, zero), axis=0)
    return pack(dot(table, both, 1, 1), roll)


def stage2(x, outer, inner, cw, sw, roll):
    n = G * 8
    g = dot(outer, jnp.concatenate(unpack(x, roll), axis=1))
    cols = []
    for f in range(2):
        re, im = (g[j * n : (j + 1) * n, f * LANES : (f + 1) * LANES] for j in range(2))
        h = jnp.concatenate((re * cw + im * sw, im * cw - re * sw), axis=1).astype(BF)
        o = dot(inner, h, 1, 1)
        rows = []
        for q in range(2):
            rows += swap_blocks([o[8 * i : 8 * i + 8, q * LANES : (q + 1) * LANES] for i in range(16)], roll)
        cols.append(jnp.concatenate(rows, axis=0))
    return jnp.concatenate(cols, axis=1).astype(BF)


def stage3(x, forward_y, back_y, total):
    c = dot(forward_y, x)
    hat = jnp.concatenate(
        (c[:, :LANES] / (-total), c[:, LANES:] / (1.0 + DIFFUSION * total)), axis=1
    ).astype(BF)
    return dot(back_y, hat).astype(BF)


def stage4(x, outer, inner, cw, sw, roll):
    x = x.astype(F32)
    parts = []
    for f in range(2):
        tiles = [x[8 * r : 8 * r + 8, f * LANES : (f + 1) * LANES] for r in range(G)]
        halves = [jnp.concatenate(swap_blocks(tiles[16 * q : 16 * q + 16], roll), axis=0) for q in range(2)]
        v = jnp.concatenate(halves, axis=1).astype(BF)
        h = dot(v, inner, 0, 0)
        re, im = h[:, :LANES], h[:, LANES:]
        parts.append(jnp.concatenate((re * cw - im * sw, im * cw + re * sw), axis=0).astype(BF))
    return pack(dot(outer, jnp.concatenate(parts, axis=1)), roll)


def stage5(x, table, roll):
    return tuple(dot(v, table, 0, 0)[: ZL * YL].astype(BF) for v in unpack(x, roll))


def call(fn, out, *args):
    outs = out if isinstance(out, list) else [out]
    single = outs is not out

    def kernel(*refs):
        result = fn(*(r[...] for r in refs[: len(args)]))
        for ref, value in zip(refs[len(args) :], (result,) if single else result, strict=True):
            ref[...] = value

    vmem = pl.BlockSpec(memory_space=pltpu.VMEM)
    shapes = tuple(jax.ShapeDtypeStruct(s, BF) for s in outs)
    result = pl.pallas_call(
        kernel,
        out_shape=shapes,
        in_specs=[vmem] * len(args),
        out_specs=(vmem,) * len(outs),
        name=fn.__name__,
    )(*args)
    return result[0] if single else result


def wave_numbers(row_at, col_at):
    lane = lax.iota(jnp.int32, LANES)
    k = lane % 8
    t = lane // 8 % WAVES
    m = col_at * PER + k
    n = row_at + G * t
    signed = jnp.where(t < WAVES // 2, n, n - KEEP)
    kx_sq = (m.astype(F32) * (2.0 * math.pi / NX)) ** 2
    kz_sq = (signed.astype(F32) * (2.0 * math.pi / NZ)) ** 2
    return kz_sq + kx_sq


def shards(pressure_rhs, scalar_source, forward_y, back_y, wall_rates):
    fwd_x, back_x = (jnp.asarray(t, BF) for t in x_tables())
    outer_f, outer_b = jnp.asarray(z_outer(-1), BF), jnp.asarray(z_outer_back(), BF)
    inner_f, inner_b = jnp.asarray(z_inner(-1), BF), jnp.asarray(z_inner(1), BF)
    cw, sw = (jnp.asarray(t, F32) for t in twiddles())
    total = wall_rates[:, None] + wave_numbers(lax.axis_index("row"), lax.axis_index("col"))[None, :]
    roll = pltpu.roll

    def exchange(x, axis):
        shape = x.shape
        x = x.reshape(G, -1, shape[1])
        return lax.all_to_all(x, axis, split_axis=0, concat_axis=0, tiled=True).reshape(shape)

    def s1(*a):
        return stage1(*a, roll)

    def s2(*a):
        return stage2(*a, roll)

    def s4(*a):
        return stage4(*a, roll)

    def s5(*a):
        return stage5(*a, roll)

    flat = (ZL * YL, NX)
    x = call(s1, (G * 24, LANES), pressure_rhs.reshape(flat), scalar_source.reshape(flat), fwd_x)
    x = exchange(x, "col")
    x = call(s2, (NY, 2 * LANES), x, outer_f, inner_f, cw, sw)
    x = exchange(x, "row")
    x = call(stage3, (NY, 2 * LANES), x, forward_y, back_y, total)
    x = exchange(x, "row")
    x = call(s4, (G * 24, LANES), x, outer_b, inner_b, cw, sw)
    x = exchange(x, "col")
    outs = call(s5, [flat, flat], x, back_x)
    return tuple(o.reshape(ZL, YL, NX) for o in outs)


def solution(mesh):
    field = P("col", "row", None)
    return jax.shard_map(
        shards,
        mesh=mesh,
        in_specs=(field, field, P(), P(), P()),
        out_specs=(field, field),
        check_vma=False,
    )
```

profile of v0, /device:TPU:1, one launch (start us, length us, event | category | flops | bytes accessed | tf_op | source)
XLA Modules:
  0.0 111.9 jit_solution(3162945550388777331)
XLA Ops:
  0.6 2.1 %s1_.1 = bf16[768,128]{1,0:T(8,128)(2,1)} custom-call(bf16[96,384]{1,0:T(8,128)(2,1)} %bitcast.20, bf16[96,384]{1,0:T(8,128)(2,1)} %bitcast.21, bf16[512,384]{1,0:T(8,128)(2,1)} %constant.68.clone.refs_2_), custom_call_target="tpu_custom_call" | custom-call | tf_op jit(solution)/shard_map/s1/pallas_call | solution.py:184
  2.7 23.2 %all_to_all.20 = bf16[32,24,128]{2,1,0:T(8,128)(2,1)} all-to-all(bf16[32,24,128]{2,1,0:T(8,128)(2,1)} %bitcast.15), channel_id=1, replica_groups=mesh['row'=32,'col'=32] {'col'}, dimensions={0} | all-to-all | bytes 393216 | tf_op jit(solution)/shard_map/all_to_all | solution.py:217
  25.9 2.7 %s2_.1 = bf16[256,256]{1,0:T(8,128)(2,1)} custom-call(bf16[768,128]{1,0:T(8,128)(2,1)} %bitcast.13, bf16[512,512]{1,0:T(8,128)(2,1)} %constant.70.clone.refs_1_, bf16[128,256]{1,0:T(8,128)(2,1)} %constant.72.clone.refs_2_, f32[256,128]{1,0:T(8,128)} %constant.73.clone.refs_3_, f32[256,128]{1,0:T(8,128)} %constant.74.clone.refs_4_), custom_call_target="tpu_custom_call" | custom-call | tf_op jit(solution)/shard_map/s2/pallas_call | solution.py:184
  28.6 21.0 %all-to-all-start.1 = ((bf16[32,8,256]{2,1,0:T(8,128)(2,1)}), bf16[32,8,256]{2,1,0:T(8,128)(2,1)S(1)}, u32[]{:S(2)}, u32[]{:S(2)}) async-start(bf16[32,8,256]{2,1,0:T(8,128)(2,1)} %bitcast.17), calls=%async_computation.1 | async-start | bytes 262144 | tf_op jit(solution)/shard_map/all_to_all | solution.py:217
  49.6 0.0 copy-start.1
  49.6 0.7 copy-done.1
  50.3 0.8 broadcast_add_fusion.refs_3_
  51.0 15.3 %all-to-all-done.1 = bf16[32,8,256]{2,1,0:T(8,128)(2,1)S(1)} async-done(((bf16[32,8,256]{2,1,0:T(8,128)(2,1)}), bf16[32,8,256]{2,1,0:T(8,128)(2,1)S(1)}, u32[]{:S(2)}, u32[]{:S(2)}) %all-to-all-start.1) | async-done | bytes 131104 | tf_op jit(solution)/shard_map/all_to_all | solution.py:217
  66.3 0.0 copy-start
  66.3 0.6 copy-done
  67.0 2.1 %stage3.1 = bf16[256,256]{1,0:T(8,128)(2,1)} custom-call(bf16[256,256]{1,0:T(8,128)(2,1)} %bitcast.16, bf16[256,256]{1,0:T(8,128)(2,1)} %refs_1_.4, bf16[256,256]{1,0:T(8,128)(2,1)} %refs_2_.4, f32[256,128]{1,0:T(8,128)} %broadcast_add_fusion.refs_3_), custom_call_target="tpu_custom_call" | custom-call | tf_op jit(solution)/shard_map/stage3/pallas_call | solution.py:184
  69.1 22.4 %all_to_all.21 = bf16[32,8,256]{2,1,0:T(8,128)(2,1)} all-to-all(bf16[32,8,256]{2,1,0:T(8,128)(2,1)} %bitcast.19), channel_id=1, replica_groups=mesh['row'=32,'col'=32] {'row'}, dimensions={0} | all-to-all | bytes 262144 | tf_op jit(solution)/shard_map/all_to_all | solution.py:217
  91.5 2.7 %s4_.1 = bf16[768,128]{1,0:T(8,128)(2,1)} custom-call(bf16[256,256]{1,0:T(8,128)(2,1)} %bitcast.18, bf16[512,512]{1,0:T(8,128)(2,1)} %constant.71.clone.refs_1_, bf16[128,256]{1,0:T(8,128)(2,1)} %constant.72.clone.refs_2_, f32[256,128]{1,0:T(8,128)} %constant.73.clone.refs_3_, f32[256,128]{1,0:T(8,128)} %constant.74.clone.refs_4_), custom_call_target="tpu_custom_call" | custom-call | tf_op jit(solution)/shard_map/s4/pallas_call | solution.py:184
  94.1 15.7 %all_to_all.22 = bf16[32,24,128]{2,1,0:T(8,128)(2,1)} all-to-all(bf16[32,24,128]{2,1,0:T(8,128)(2,1)} %bitcast.12), channel_id=1, replica_groups=mesh['row'=32,'col'=32] {'col'}, dimensions={0} | all-to-all | bytes 393216 | tf_op jit(solution)/shard_map/all_to_all | solution.py:217
  109.8 2.1 %s5.1 = (bf16[96,384]{1,0:T(8,128)(2,1)}, bf16[96,384]{1,0:T(8,128)(2,1)}) custom-call(bf16[768,128]{1,0:T(8,128)(2,1)} %bitcast.14, bf16[512,384]{1,0:T(8,128)(2,1)} %constant.69.clone.refs_1_), custom_call_target="tpu_custom_call" | custom-call | tf_op jit(solution)/shard_map/s5/pallas_call | solution.py:184
  (1 shorter events, 0.0 us)
Async XLA Ops:
  28.6 37.7 %all-to-all-start.1 = ((bf16[32,8,256]{2,1,0:T(8,128)(2,1)}), bf16[32,8,256]{2,1,0:T(8,128)(2,1)S(1)}, u32[]{:S(2)}, u32[]{:S(2)}) async-start(bf16[32,8,256]{2,1,0:T(8,128)(2,1)} %bitcast.17), calls=%async_computation.1 | async-start | bytes 262144 | tf_op jit(solution)/shard_map/all_to_all | solution.py:217
  49.6 0.7 copy-start.1
  66.3 0.6 copy-start
where the time goes:
time: 112 us
  blocking collectives  61.2 us (55%)
  starting transfers between devices  21 us (19%)
  waiting for transfers between devices  15.3 us (14%)
  Pallas kernels  11.7 us (10%)
  local copies, waits for them, and re-layouts  1.31 us (1%)
    all_to_all x3, blocking collectives, exchange(): lax.all_to_all(x, axis, split_axis=0, concat_axis=0, tiled=True)  61.2 us
    all_to_all x1, starting transfers between devices, exchange(): lax.all_to_all(x, axis, split_axis=0, concat_axis=0, tiled=True)  21 us
    all_to_all x1, waiting for transfers between devices, exchange(): lax.all_to_all(x, axis, split_axis=0, concat_axis=0, tiled=True)  15.3 us
    pallas_call x5, Pallas kernels, call(): pl.pallas_call(kernel, out_shape=shapes, in_specs=[vmem] * len(args), out...  11.7 us
  transfers between devices with their start and end apart: 1, of which 1 were waited for; matrix products, arithmetic and copies ran while one was open for 1% of the time, Pallas kernels for 0%

commit v1 on v0

--- a/solution.py
+++ b/solution.py
@@ -170,7 +170,7 @@
     return tuple(dot(v, table, 0, 0)[: ZL * YL].astype(BF) for v in unpack(x, roll))
 
 
-def call(fn, out, *args):
+def call(fn, out, *args, fast=(True, True)):
     outs = out if isinstance(out, list) else [out]
     single = outs is not out
 
@@ -180,7 +180,10 @@
             ref[...] = value
 
     vmem = pl.BlockSpec(memory_space=pltpu.VMEM)
-    shapes = tuple(jax.ShapeDtypeStruct(s, BF) for s in outs)
+    make = pltpu.VMEM if fast[1] else jax.ShapeDtypeStruct
+    shapes = tuple(make(s, BF) for s in outs)
+    if fast[0]:
+        args = [pltpu.with_memory_space_constraint(a, pltpu.VMEM) for a in args]
     result = pl.pallas_call(
         kernel,
         out_shape=shapes,
@@ -229,15 +232,16 @@
         return stage5(*a, roll)
 
     flat = (ZL * YL, NX)
-    x = call(s1, (G * 24, LANES), pressure_rhs.reshape(flat), scalar_source.reshape(flat), fwd_x)
+    x = call(s1, (G * 24, LANES), pressure_rhs.reshape(flat), scalar_source.reshape(flat), fwd_x, fast=(False, True))
     x = exchange(x, "col")
     x = call(s2, (NY, 2 * LANES), x, outer_f, inner_f, cw, sw)
+    x, total = lax.optimization_barrier((x, total))
     x = exchange(x, "row")
     x = call(stage3, (NY, 2 * LANES), x, forward_y, back_y, total)
     x = exchange(x, "row")
     x = call(s4, (G * 24, LANES), x, outer_b, inner_b, cw, sw)
     x = exchange(x, "col")
-    outs = call(s5, [flat, flat], x, back_x)
+    outs = call(s5, [flat, flat], x, back_x, fast=(True, False))
     return tuple(o.reshape(ZL, YL, NX) for o in outs)
 
 

time: 112 us -> 104 us (0.929)
  blocking collectives: 61.2 us -> 74.3 us
  starting transfers between devices: 21 us -> 13.6 us
  Pallas kernels: 11.7 us -> 5.22 us
  waiting for transfers between devices: 15.3 us -> 9.68 us
  local copies, waits for them, and re-layouts: 1.31 us -> 0.05 us
    all_to_all x3, blocking collectives: 61.2 us -> 74.3 us  [exchange(): lax.all_to_all(x, axis, split_axis=0, concat_axis=0, tiled=True)]
    all_to_all x1, starting transfers between devices: 21 us -> 13.6 us  [exchange(): lax.all_to_all(x, axis, split_axis=0, concat_axis=0, tiled=True)]
    pallas_call x5, Pallas kernels: 11.7 us -> 5.22 us  [call(): pl.pallas_call(kernel, out_shape=shapes, in_specs=[vmem] * len(args), out...]
    all_to_all x1, waiting for transfers between devices: 15.3 us -> 9.68 us  [exchange(): lax.all_to_all(x, axis, split_axis=0, concat_axis=0, tiled=True)]
    unnamed x4 -> x18, local copies, waits for them, and re-layouts: 1.31 us -> 0.05 us
  transfers between devices with their start and end apart: 1 -> 1, of which waited for: 1 -> 1; matrix products, arithmetic and copies ran while one was open for 1% -> 0% of each run, Pallas kernels for 0% -> 0%
where the time goes in v1:
time: 104 us
  blocking collectives  74.3 us (71%)
  starting transfers between devices  13.6 us (13%)
  waiting for transfers between devices  9.68 us (9%)
  Pallas kernels  5.22 us (5%)
    all_to_all x3, blocking collectives, exchange(): lax.all_to_all(x, axis, split_axis=0, concat_axis=0, tiled=True)  74.3 us
    all_to_all x1, starting transfers between devices, exchange(): lax.all_to_all(x, axis, split_axis=0, concat_axis=0, tiled=True)  13.6 us
    all_to_all x1, waiting for transfers between devices, exchange(): lax.all_to_all(x, axis, split_axis=0, concat_axis=0, tiled=True)  9.68 us
    pallas_call x5, Pallas kernels, call(): pl.pallas_call(kernel, out_shape=shapes, in_specs=[vmem] * len(args), out...  5.22 us
  transfers between devices with their start and end apart: 1, of which 1 were waited for; matrix products, arithmetic and copies ran while one was open for 0% of the time, Pallas kernels for 0%

profile of v1, /device:TPU:1, one launch (start us, length us, event | category | flops | bytes accessed | tf_op | source)
XLA Modules:
  0.0 103.7 jit_solution(14321492919505805226)
XLA Ops:
  0.6 0.0 copy-start.3
  0.6 2.1 %s1_.1 = bf16[768,128]{1,0:T(8,128)(2,1)} custom-call(bf16[96,384]{1,0:T(8,128)(2,1)} %bitcast.19, bf16[96,384]{1,0:T(8,128)(2,1)} %bitcast.20, bf16[512,384]{1,0:T(8,128)(2,1)} %constant.68.clone.refs_2_), custom_call_target="tpu_custom_call" | custom-call | tf_op jit(solution)/shard_map/s1/pallas_call | solution.py:187
  2.8 0.0 copy-start.8
  2.8 0.0 copy-start.1
  2.8 0.0 copy-start.5
  2.8 13.6 %all-to-all-start = ((bf16[32,24,128]{2,1,0:T(8,128)(2,1)}), bf16[32,24,128]{2,1,0:T(8,128)(2,1)S(1)}, u32[]{:S(2)}, u32[]{:S(2)}) async-start(bf16[32,24,128]{2,1,0:T(8,128)(2,1)} %bitcast.2), calls=%async_computation | async-start | bytes 393216 | tf_op jit(solution)/shard_map/all_to_all | solution.py:220
  16.4 0.0 copy-start
  16.4 0.0 copy-done.8
  16.4 0.1 broadcast_add_fusion.refs_3_
  16.5 9.7 %all-to-all-done = bf16[32,24,128]{2,1,0:T(8,128)(2,1)S(1)} async-done(((bf16[32,24,128]{2,1,0:T(8,128)(2,1)}), bf16[32,24,128]{2,1,0:T(8,128)(2,1)S(1)}, u32[]{:S(2)}, u32[]{:S(2)}) %all-to-all-start) | async-done | bytes 196640 | tf_op jit(solution)/shard_map/all_to_all | solution.py:220
  26.2 0.0 copy-done.3
  26.2 0.0 copy-done.1
  26.2 0.0 copy-done.5
  26.2 0.0 copy-done
  26.2 0.9 s2_.1
  27.1 0.0 copy-start.6
  27.1 0.0 copy-start.7
  27.2 37.4 %all_to_all.20 = bf16[32,8,256]{2,1,0:T(8,128)(2,1)S(1)} all-to-all(bf16[32,8,256]{2,1,0:T(8,128)(2,1)S(1)} %bitcast.16), channel_id=1, replica_groups=mesh['row'=32,'col'=32] {'row'}, dimensions={0} | all-to-all | bytes 262144 | tf_op jit(solution)/shard_map/all_to_all | solution.py:220
  64.6 0.0 copy-start.2
  64.6 0.0 copy-done.6
  64.6 0.0 copy-done.7
  64.6 0.4 stage3.1
  65.0 21.3 %all_to_all.21 = bf16[32,8,256]{2,1,0:T(8,128)(2,1)S(1)} all-to-all(bf16[32,8,256]{2,1,0:T(8,128)(2,1)S(1)} %bitcast.18), channel_id=1, replica_groups=mesh['row'=32,'col'=32] {'row'}, dimensions={0} | all-to-all | bytes 262144 | tf_op jit(solution)/shard_map/all_to_all | solution.py:220
  86.3 0.0 copy-done.2
  86.3 0.8 s4_.1
  87.1 0.0 copy-start.4
  87.1 15.6 %all_to_all.22 = bf16[32,24,128]{2,1,0:T(8,128)(2,1)S(1)} all-to-all(bf16[32,24,128]{2,1,0:T(8,128)(2,1)S(1)} %bitcast.13), channel_id=1, replica_groups=mesh['row'=32,'col'=32] {'col'}, dimensions={0} | all-to-all | bytes 393216 | tf_op jit(solution)/shard_map/all_to_all | solution.py:220
  102.7 0.0 copy-done.4
  102.7 1.0 s5.1
  (1 shorter events, 0.0 us)
Async XLA Ops:
  0.6 25.6 %copy-start.3 = (bf16[512,512]{1,0:T(8,128)(2,1)S(1)}, bf16[512,512]{1,0:T(8,128)(2,1)}, u32[]{:S(2)}) copy-start(bf16[512,512]{1,0:T(8,128)(2,1)} %constant.70.clone.refs_1_) | copy-start | bytes 1572868
  2.8 13.6 %copy-start.8 = (f32[256]{0:T(256)S(1)}, f32[256]{0:T(256)}, u32[]{:S(2)}) copy-start(f32[256]{0:T(256)} %param.17) | copy-start | bytes 3076
  2.8 23.4 %copy-start.1 = (f32[256,128]{1,0:T(8,128)S(1)}, f32[256,128]{1,0:T(8,128)}, u32[]{:S(2)}) copy-start(f32[256,128]{1,0:T(8,128)} %constant.74.clone.refs_4_) | copy-start | bytes 393220
  2.8 23.4 %copy-start.5 = (bf16[128,256]{1,0:T(8,128)(2,1)S(1)}, bf16[128,256]{1,0:T(8,128)(2,1)}, u32[]{:S(2)}) copy-start(bf16[128,256]{1,0:T(8,128)(2,1)} %constant.72.clone.refs_2_) | copy-start | bytes 196612
  2.8 23.4 %all-to-all-start = ((bf16[32,24,128]{2,1,0:T(8,128)(2,1)}), bf16[32,24,128]{2,1,0:T(8,128)(2,1)S(1)}, u32[]{:S(2)}, u32[]{:S(2)}) async-start(bf16[32,24,128]{2,1,0:T(8,128)(2,1)} %bitcast.2), calls=%async_computation | async-start | bytes 393216 | tf_op jit(solution)/shard_map/all_to_all | solution.py:220
  16.4 9.8 %copy-start = (f32[256,128]{1,0:T(8,128)S(1)}, f32[256,128]{1,0:T(8,128)}, u32[]{:S(2)}) copy-start(f32[256,128]{1,0:T(8,128)} %constant.73.clone.refs_3_) | copy-start | bytes 393220
  27.1 37.4 %copy-start.6 = (bf16[256,256]{1,0:T(8,128)(2,1)S(1)}, bf16[256,256]{1,0:T(8,128)(2,1)}, u32[]{:S(2)}) copy-start(bf16[256,256]{1,0:T(8,128)(2,1)} %refs_1_.4) | copy-start | bytes 393220
  27.1 37.4 %copy-start.7 = (bf16[256,256]{1,0:T(8,128)(2,1)S(1)}, bf16[256,256]{1,0:T(8,128)(2,1)}, u32[]{:S(2)}) copy-start(bf16[256,256]{1,0:T(8,128)(2,1)} %refs_2_.4) | copy-start | bytes 393220
  64.6 21.7 %copy-start.2 = (bf16[512,512]{1,0:T(8,128)(2,1)S(1)}, bf16[512,512]{1,0:T(8,128)(2,1)}, u32[]{:S(2)}) copy-start(bf16[512,512]{1,0:T(8,128)(2,1)} %constant.71.clone.refs_1_) | copy-start | bytes 1572868
  87.1 15.7 %copy-start.4 = (bf16[512,384]{1,0:T(8,128)(2,1)S(1)}, bf16[512,384]{1,0:T(8,128)(2,1)}, u32[]{:S(2)}) copy-start(bf16[512,384]{1,0:T(8,128)(2,1)} %constant.69.clone.refs_1_) | copy-start | bytes 1179652

commit v2 on v1

--- a/solution.py
+++ b/solution.py
@@ -145,7 +145,8 @@
     return jnp.concatenate(cols, axis=1).astype(BF)
 
 
-def stage3(x, forward_y, back_y, total):
+def stage3(x, forward_y, back_y, wall, row_at, col_at):
+    total = jnp.broadcast_to(wall, (LANES, NY)).T + wave_numbers(row_at, col_at)
     c = dot(forward_y, x)
     hat = jnp.concatenate(
         (c[:, :LANES] / (-total), c[:, LANES:] / (1.0 + DIFFUSION * total)), axis=1
@@ -195,7 +196,7 @@
 
 
 def wave_numbers(row_at, col_at):
-    lane = lax.iota(jnp.int32, LANES)
+    lane = lax.broadcasted_iota(jnp.int32, (1, LANES), 1)
     k = lane % 8
     t = lane // 8 % WAVES
     m = col_at * PER + k
@@ -211,7 +212,6 @@
     outer_f, outer_b = jnp.asarray(z_outer(-1), BF), jnp.asarray(z_outer_back(), BF)
     inner_f, inner_b = jnp.asarray(z_inner(-1), BF), jnp.asarray(z_inner(1), BF)
     cw, sw = (jnp.asarray(t, F32) for t in twiddles())
-    total = wall_rates[:, None] + wave_numbers(lax.axis_index("row"), lax.axis_index("col"))[None, :]
     roll = pltpu.roll
 
     def exchange(x, axis):
@@ -225,6 +225,9 @@
     def s2(*a):
         return stage2(*a, roll)
 
+    def s3(*a):
+        return stage3(*a, lax.axis_index("row"), lax.axis_index("col"))
+
     def s4(*a):
         return stage4(*a, roll)
 
@@ -235,9 +238,8 @@
     x = call(s1, (G * 24, LANES), pressure_rhs.reshape(flat), scalar_source.reshape(flat), fwd_x, fast=(False, True))
     x = exchange(x, "col")
     x = call(s2, (NY, 2 * LANES), x, outer_f, inner_f, cw, sw)
-    x, total = lax.optimization_barrier((x, total))
     x = exchange(x, "row")
-    x = call(stage3, (NY, 2 * LANES), x, forward_y, back_y, total)
+    x = call(s3, (NY, 2 * LANES), x, forward_y, back_y, wall_rates.reshape(1, NY))
     x = exchange(x, "row")
     x = call(s4, (G * 24, LANES), x, outer_b, inner_b, cw, sw)
     x = exchange(x, "col")

time: 104 us -> 103 us (level)
  blocking collectives: 74.3 us -> 97.5 us
  starting transfers between devices: 13.6 us -> 0 us
  waiting for transfers between devices: 9.68 us -> 0 us
    all_to_all x3 -> x4, blocking collectives: 74.3 us -> 97.5 us  [exchange(): lax.all_to_all(x, axis, split_axis=0, concat_axis=0, tiled=True)]
    all_to_all x1 -> x0, starting transfers between devices: 13.6 us -> none  [exchange(): lax.all_to_all(x, axis, split_axis=0, concat_axis=0, tiled=True)]
    all_to_all x1 -> x0, waiting for transfers between devices: 9.68 us -> none  [exchange(): lax.all_to_all(x, axis, split_axis=0, concat_axis=0, tiled=True)]
  transfers between devices with their start and end apart: 1 -> 0, of which waited for: 1 -> 0; matrix products, arithmetic and copies ran while one was open for 0% -> 0% of each run, Pallas kernels for 0% -> 0%
where the time goes in v2:
time: 103 us
  blocking collectives  97.5 us (95%)
  Pallas kernels  4.54 us (4%)
    all_to_all x4, blocking collectives, exchange(): lax.all_to_all(x, axis, split_axis=0, concat_axis=0, tiled=True)  97.5 us
    pallas_call x5, Pallas kernels, call(): pl.pallas_call(kernel, out_shape=shapes, in_specs=[vmem] * len(args), out...  4.54 us

profile of v2, /device:TPU:1, one launch (start us, length us, event | category | flops | bytes accessed | tf_op | source)
XLA Modules:
  0.0 102.9 jit_solution(3357908135697185923)
XLA Ops:
  0.6 0.0 copy-start.3
  0.6 1.5 %s1_.1 = bf16[768,128]{1,0:T(8,128)(2,1)S(1)} custom-call(bf16[96,384]{1,0:T(8,128)(2,1)} %bitcast.22, bf16[96,384]{1,0:T(8,128)(2,1)} %bitcast.23, bf16[512,384]{1,0:T(8,128)(2,1)} %constant.14.clone.refs_2_), custom_call_target="tpu_custom_call" | custom-call | tf_op jit(solution)/shard_map/s1/pallas_call | solution.py:188
  2.1 0.0 copy-start
  2.1 0.0 copy-start.1
  2.1 0.0 copy-start.5
  2.1 23.0 %all_to_all.20 = bf16[32,24,128]{2,1,0:T(8,128)(2,1)S(1)} all-to-all(bf16[32,24,128]{2,1,0:T(8,128)(2,1)S(1)} %bitcast.16), channel_id=1, replica_groups=mesh['row'=32,'col'=32] {'col'}, dimensions={0} | all-to-all | bytes 393216 | tf_op jit(solution)/shard_map/all_to_all | solution.py:220
  25.1 0.0 copy-done.3
  25.1 0.0 copy-done
  25.1 0.0 copy-done.1
  25.1 0.0 copy-done.5
  25.2 0.0 copy-start.6
  25.2 0.0 copy-start.7
  25.2 0.0 copy-start.8
  25.2 0.9 s2_.1
  26.1 0.0 copy-start.2
  26.1 37.6 %all_to_all.21 = bf16[32,8,256]{2,1,0:T(8,128)(2,1)S(1)} all-to-all(bf16[32,8,256]{2,1,0:T(8,128)(2,1)S(1)} %bitcast.18), channel_id=1, replica_groups=mesh['row'=32,'col'=32] {'row'}, dimensions={0} | all-to-all | bytes 262144 | tf_op jit(solution)/shard_map/all_to_all | solution.py:220
  63.7 0.0 copy-done.6
  63.7 0.0 copy-done.7
  63.7 0.0 copy-done.8
  63.7 0.4 s3.1
  64.2 21.3 %all_to_all.22 = bf16[32,8,256]{2,1,0:T(8,128)(2,1)S(1)} all-to-all(bf16[32,8,256]{2,1,0:T(8,128)(2,1)S(1)} %bitcast.20), channel_id=1, replica_groups=mesh['row'=32,'col'=32] {'row'}, dimensions={0} | all-to-all | bytes 262144 | tf_op jit(solution)/shard_map/all_to_all | solution.py:220
  85.4 0.0 copy-done.2
  85.4 0.8 s4_.1
  86.3 0.0 copy-start.4
  86.3 15.7 %all_to_all.23 = bf16[32,24,128]{2,1,0:T(8,128)(2,1)S(1)} all-to-all(bf16[32,24,128]{2,1,0:T(8,128)(2,1)S(1)} %bitcast.13), channel_id=1, replica_groups=mesh['row'=32,'col'=32] {'col'}, dimensions={0} | all-to-all | bytes 393216 | tf_op jit(solution)/shard_map/all_to_all | solution.py:220
  101.9 0.0 copy-done.4
  101.9 1.0 s5.1
Async XLA Ops:
  0.6 24.5 %copy-start.3 = (bf16[512,512]{1,0:T(8,128)(2,1)S(1)}, bf16[512,512]{1,0:T(8,128)(2,1)}, u32[]{:S(2)}) copy-start(bf16[512,512]{1,0:T(8,128)(2,1)} %constant.16.clone.refs_1_) | copy-start | bytes 1572868
  2.1 23.0 %copy-start = (f32[256,128]{1,0:T(8,128)S(1)}, f32[256,128]{1,0:T(8,128)}, u32[]{:S(2)}) copy-start(f32[256,128]{1,0:T(8,128)} %constant.20.clone.refs_4_) | copy-start | bytes 393220
  2.1 23.0 %copy-start.1 = (f32[256,128]{1,0:T(8,128)S(1)}, f32[256,128]{1,0:T(8,128)}, u32[]{:S(2)}) copy-start(f32[256,128]{1,0:T(8,128)} %constant.19.clone.refs_3_) | copy-start | bytes 393220
  2.1 23.0 %copy-start.5 = (bf16[128,256]{1,0:T(8,128)(2,1)S(1)}, bf16[128,256]{1,0:T(8,128)(2,1)}, u32[]{:S(2)}) copy-start(bf16[128,256]{1,0:T(8,128)(2,1)} %constant.18.clone.refs_2_) | copy-start | bytes 196612
  25.2 38.6 %copy-start.6 = (bf16[256,256]{1,0:T(8,128)(2,1)S(1)}, bf16[256,256]{1,0:T(8,128)(2,1)}, u32[]{:S(2)}) copy-start(bf16[256,256]{1,0:T(8,128)(2,1)} %refs_1_.4) | copy-start | bytes 393220
  25.2 38.6 %copy-start.7 = (bf16[256,256]{1,0:T(8,128)(2,1)S(1)}, bf16[256,256]{1,0:T(8,128)(2,1)}, u32[]{:S(2)}) copy-start(bf16[256,256]{1,0:T(8,128)(2,1)} %refs_2_.4) | copy-start | bytes 393220
  25.2 38.6 %copy-start.8 = (f32[256]{0:T(256)S(1)}, f32[256]{0:T(256)}, u32[]{:S(2)}) copy-start(f32[256]{0:T(256)} %param.17) | copy-start | bytes 3076
  26.1 59.3 %copy-start.2 = (bf16[512,512]{1,0:T(8,128)(2,1)S(1)}, bf16[512,512]{1,0:T(8,128)(2,1)}, u32[]{:S(2)}) copy-start(bf16[512,512]{1,0:T(8,128)(2,1)} %constant.17.clone.refs_1_) | copy-start | bytes 1572868
  86.3 15.7 %copy-start.4 = (bf16[512,384]{1,0:T(8,128)(2,1)S(1)}, bf16[512,384]{1,0:T(8,128)(2,1)}, u32[]{:S(2)}) copy-start(bf16[512,384]{1,0:T(8,128)(2,1)} %constant.15.clone.refs_1_) | copy-start | bytes 1179652

commit v3 on v2

--- a/solution.py
+++ b/solution.py
@@ -51,24 +51,32 @@
     return fwd.reshape(-1, NX), back.reshape(-1, NX)
 
 
+def waves(table, axis):
+    shape = list(table.shape)
+    shape[axis : axis + 2] = [2, G // 2 * PER]
+    pad = [(0, 0)] * len(shape)
+    pad[axis + 1] = (0, LANES - shape[axis + 1])
+    return np.pad(table.reshape(shape), pad)
+
+
 def z_outer(sign):
-    out = np.zeros((2, G, 8, 2, G, 8))
+    out = np.zeros((2, G, PER, 2, G, 8))
     angle = 2.0 * math.pi * (np.outer(np.arange(G), np.arange(G)) % G) / G
     cos, sin = np.cos(angle) / math.sqrt(G), np.sin(angle) / math.sqrt(G)
     for h, i, p, k in items():
         for q in range(2):
             out[q, :, k, h, :, i] = pairs(q, p, cos, sin, sign)
-    return out.reshape(2 * G * 8, 2 * G * 8)
+    return waves(out, 1).reshape(4 * LANES, 2 * G * 8)
 
 
 def z_outer_back():
-    out = np.zeros((2, G, 8, 2, G, 8))
+    out = np.zeros((2, G, 8, 2, G, PER))
     angle = 2.0 * math.pi * (np.outer(np.arange(G), np.arange(G)) % G) / G
     cos, sin = np.cos(angle) / math.sqrt(G), np.sin(angle) / math.sqrt(G)
     for h, i, p, k in items():
         for q in range(2):
             out[h, :, i, q, :, k] = pairs(p, q, cos, sin, 1)
-    return out.reshape(2 * G * 8, 2 * G * 8)
+    return waves(out, 4).reshape(2 * G * 8, 4 * LANES)
 
 
 def z_inner(sign):
@@ -85,9 +93,9 @@
 
 def twiddles():
     angle = 2.0 * math.pi * np.outer(np.arange(G), np.arange(ZL)) / NZ
-    angle = np.repeat(np.repeat(angle, 8, axis=0), YL, axis=1)
-    pad = LANES - ZL * YL
-    return np.pad(np.cos(angle), ((0, 0), (0, pad))), np.pad(np.sin(angle), ((0, 0), (0, pad)))
+    angle = np.repeat(np.repeat(angle, PER, axis=0).reshape(G, PER, ZL), YL, axis=2)
+    angle = np.pad(waves(angle, 0).reshape(2 * LANES, ZL * YL), ((0, 0), (0, LANES - ZL * YL)))
+    return np.cos(angle), np.sin(angle)
 
 
 def dot(a, b, ca=1, cb=0):
@@ -112,16 +120,44 @@
 
 
 def swap_blocks(rows, roll):
-    lane = lax.broadcasted_iota(jnp.int32, (8, LANES), 1) // 8
+    lane = lax.broadcasted_iota(jnp.int32, (8, LANES), 1) // PER
     x = list(rows)
     for d in (8, 4, 2, 1):
         high = (lane & d) != 0
         for i in range(16):
             if not i & d:
                 a, b = x[i], x[i + d]
-                x[i] = jnp.where(high, roll(b, 8 * d, 1), a)
-                x[i + d] = jnp.where(high, b, roll(a, LANES - 8 * d, 1))
+                x[i] = jnp.where(high, roll(b, PER * d, 1), a)
+                x[i + d] = jnp.where(high, b, roll(a, LANES - PER * d, 1))
     return x
+
+
+def fold(z, roll):
+    lane = lax.broadcasted_iota(jnp.int32, (NY, LANES), 1)
+    moved = roll(z[1], LANES - LANES // 4, 1)
+    whole = jnp.where(lane < 3 * LANES // 4, z[0], moved).reshape(G, YL, LANES)
+    low = moved.reshape(G, YL, LANES)[:, :4]
+    high = roll(moved, LANES // 2, 1).reshape(G, YL, LANES)[:, 4:]
+    lane = lax.broadcasted_iota(jnp.int32, (G, 4, LANES), 2)
+    rest = jnp.where(lane < LANES // 2, low, high)
+    return jnp.concatenate((whole[:, :4], whole[:, 4:], rest), axis=2).astype(BF)
+
+
+def unfold(x, roll):
+    x = x.astype(F32)
+    rest = x[:, :, 2 * LANES :]
+    whole = jnp.concatenate((x[:, :, :LANES], x[:, :, LANES : 2 * LANES]), axis=1).reshape(NY, LANES)
+    rest = jnp.concatenate((rest, roll(rest, LANES // 2, 2)), axis=1).reshape(NY, LANES)
+    return whole, rest
+
+
+def refold(whole, rest, roll):
+    lane = lax.broadcasted_iota(jnp.int32, (G, 4, LANES), 2)
+    low = rest.reshape(G, YL, LANES)[:, :4]
+    high = roll(rest, LANES // 2, 1).reshape(G, YL, LANES)[:, 4:]
+    whole = whole.reshape(G, YL, LANES)
+    rest = jnp.where(lane < LANES // 2, low, high)
+    return jnp.concatenate((whole[:, :4], whole[:, 4:], rest), axis=2).astype(BF)
 
 
 def stage1(p, s, table, roll):
@@ -142,23 +178,28 @@
         for q in range(2):
             rows += swap_blocks([o[8 * i : 8 * i + 8, q * LANES : (q + 1) * LANES] for i in range(16)], roll)
         cols.append(jnp.concatenate(rows, axis=0))
-    return jnp.concatenate(cols, axis=1).astype(BF)
-
-
-def stage3(x, forward_y, back_y, wall, row_at, col_at):
-    total = jnp.broadcast_to(wall, (LANES, NY)).T + wave_numbers(row_at, col_at)
-    c = dot(forward_y, x)
-    hat = jnp.concatenate(
-        (c[:, :LANES] / (-total), c[:, LANES:] / (1.0 + DIFFUSION * total)), axis=1
-    ).astype(BF)
-    return dot(back_y, hat).astype(BF)
+    return fold(cols, roll)
+
+
+def stage3(x, forward_y, back_y, wall, row_at, col_at, roll):
+    wall = jnp.broadcast_to(wall, (LANES, NY)).T
+    lane = lax.broadcasted_iota(jnp.int32, (1, LANES), 1)
+    c = dot(forward_y, jnp.concatenate(unfold(x, roll), axis=1).astype(BF))
+    total = wall + wave_numbers(jnp.where(lane < 96, lane, lane - 96), row_at, col_at)
+    scale = jnp.where(lane < 96, -total, 1.0 + DIFFUSION * total)
+    rest = 1.0 + DIFFUSION * (wall + wave_numbers(lane % 64 + 32, row_at, col_at))
+    hat = jnp.concatenate((c[:, :LANES] / scale, c[:, LANES:] / rest), axis=1).astype(BF)
+    e = dot(back_y, hat)
+    return refold(e[:, :LANES], e[:, LANES:], roll)
 
 
 def stage4(x, outer, inner, cw, sw, roll):
-    x = x.astype(F32)
+    whole, rest = unfold(x, roll)
+    lane = lax.broadcasted_iota(jnp.int32, (NY, LANES), 1)
+    second = jnp.where(lane < LANES // 4, roll(whole, LANES // 4, 1), roll(rest, LANES // 4, 1))
     parts = []
-    for f in range(2):
-        tiles = [x[8 * r : 8 * r + 8, f * LANES : (f + 1) * LANES] for r in range(G)]
+    for z in (whole, second):
+        tiles = [z[8 * r : 8 * r + 8] for r in range(G)]
         halves = [jnp.concatenate(swap_blocks(tiles[16 * q : 16 * q + 16], roll), axis=0) for q in range(2)]
         v = jnp.concatenate(halves, axis=1).astype(BF)
         h = dot(v, inner, 0, 0)
@@ -195,10 +236,9 @@
     return result[0] if single else result
 
 
-def wave_numbers(row_at, col_at):
-    lane = lax.broadcasted_iota(jnp.int32, (1, LANES), 1)
-    k = lane % 8
-    t = lane // 8 % WAVES
+def wave_numbers(lane, row_at, col_at):
+    k = lane % PER
+    t = lane // PER % WAVES
     m = col_at * PER + k
     n = row_at + G * t
     signed = jnp.where(t < WAVES // 2, n, n - KEEP)
@@ -216,7 +256,7 @@
 
     def exchange(x, axis):
         shape = x.shape
-        x = x.reshape(G, -1, shape[1])
+        x = x.reshape(G, -1, shape[-1])
         return lax.all_to_all(x, axis, split_axis=0, concat_axis=0, tiled=True).reshape(shape)
 
     def s1(*a):
@@ -226,7 +266,7 @@
         return stage2(*a, roll)
 
     def s3(*a):
-        return stage3(*a, lax.axis_index("row"), lax.axis_index("col"))
+        return stage3(*a, lax.axis_index("row"), lax.axis_index("col"), roll)
 
     def s4(*a):
         return stage4(*a, roll)
@@ -237,9 +277,9 @@
     flat = (ZL * YL, NX)
     x = call(s1, (G * 24, LANES), pressure_rhs.reshape(flat), scalar_source.reshape(flat), fwd_x, fast=(False, True))
     x = exchange(x, "col")
-    x = call(s2, (NY, 2 * LANES), x, outer_f, inner_f, cw, sw)
+    x = call(s2, (G, 4, 3 * LANES), x, outer_f, inner_f, cw, sw)
     x = exchange(x, "row")
-    x = call(s3, (NY, 2 * LANES), x, forward_y, back_y, wall_rates.reshape(1, NY))
+    x = call(s3, (G, 4, 3 * LANES), x, forward_y, back_y, wall_rates.reshape(1, NY))
     x = exchange(x, "row")
     x = call(s4, (G * 24, LANES), x, outer_b, inner_b, cw, sw)
     x = exchange(x, "col")

time: 103 us -> 101 us (0.981)
  blocking collectives: 97.5 us -> 94.8 us
    all_to_all x4, blocking collectives: 97.5 us -> 94.8 us  [exchange(): lax.all_to_all(x, axis, split_axis=0, concat_axis=0, tiled=True)]
where the time goes in v3:
time: 101 us
  blocking collectives  94.8 us (94%)
  Pallas kernels  5 us (5%)
    all_to_all x4, blocking collectives, exchange(): lax.all_to_all(x, axis, split_axis=0, concat_axis=0, tiled=True)  94.8 us
    pallas_call x5, Pallas kernels, call(): pl.pallas_call(kernel, out_shape=shapes, in_specs=[vmem] * len(args), out...  5 us

profile of v3, /device:TPU:1, one launch (start us, length us, event | category | flops | bytes accessed | tf_op | source)
XLA Modules:
  0.0 100.6 jit_solution(13633603492785812594)
XLA Ops:
  0.6 0.0 copy-start.3
  0.6 1.5 %s1_.1 = bf16[768,128]{1,0:T(8,128)(2,1)S(1)} custom-call(bf16[96,384]{1,0:T(8,128)(2,1)} %bitcast.14, bf16[96,384]{1,0:T(8,128)(2,1)} %bitcast.15, bf16[512,384]{1,0:T(8,128)(2,1)} %constant.14.clone.refs_2_), custom_call_target="tpu_custom_call" | custom-call | tf_op jit(solution)/shard_map/s1/pallas_call | solution.py:229
  2.1 0.0 copy-start
  2.1 0.0 copy-start.1
  2.1 0.0 copy-start.5
  2.1 23.0 %all_to_all.20 = bf16[32,24,128]{2,1,0:T(8,128)(2,1)S(1)} all-to-all(bf16[32,24,128]{2,1,0:T(8,128)(2,1)S(1)} %bitcast.12), channel_id=1, replica_groups=mesh['row'=32,'col'=32] {'col'}, dimensions={0} | all-to-all | bytes 393216 | tf_op jit(solution)/shard_map/all_to_all | solution.py:260
  25.1 0.0 copy-done.3
  25.1 0.0 copy-done
  25.1 0.0 copy-done.1
  25.1 0.0 copy-done.5
  25.2 0.0 copy-start.6
  25.2 0.0 copy-start.7
  25.2 0.0 copy-start.8
  25.2 1.1 %s2_.1 = bf16[32,4,384]{2,1,0:T(4,128)(2,1)S(1)} custom-call(bf16[768,128]{1,0:T(8,128)(2,1)S(1)} %bitcast.10, bf16[512,512]{1,0:T(8,128)(2,1)S(1)} %copy-done.3, bf16[128,256]{1,0:T(8,128)(2,1)S(1)} %copy-done.5, f32[256,128]{1,0:T(8,128)S(1)} %copy-done.1, f32[256,128]{1,0:T(8,128)S(1)} %copy-done), custom_call_target="tpu_custom_call" | custom-call | tf_op jit(solution)/shard_map/s2/pallas_call | solution.py:229
  26.3 0.0 copy-start.2
  26.3 36.5 %all_to_all.21.refs_0_ = bf16[32,4,384]{2,1,0:T(4,128)(2,1)S(1)} all-to-all(bf16[32,4,384]{2,1,0:T(4,128)(2,1)S(1)} %s2_.1), channel_id=1, replica_groups=mesh['row'=32,'col'=32] {'row'}, dimensions={0} | all-to-all | bytes 196608 | tf_op jit(solution)/shard_map/all_to_all | solution.py:260
  62.8 0.0 copy-done.6
  62.8 0.0 copy-done.7
  62.8 0.0 copy-done.8
  62.8 0.5 s3.1
  63.3 20.1 %all_to_all.22.refs_0_ = bf16[32,4,384]{2,1,0:T(4,128)(2,1)S(1)} all-to-all(bf16[32,4,384]{2,1,0:T(4,128)(2,1)S(1)} %s3.1), channel_id=1, replica_groups=mesh['row'=32,'col'=32] {'row'}, dimensions={0} | all-to-all | bytes 196608 | tf_op jit(solution)/shard_map/all_to_all | solution.py:260
  83.4 0.0 copy-done.2
  83.4 1.0 s4_.1
  84.4 0.0 copy-start.4
  84.5 15.2 %all_to_all.23 = bf16[32,24,128]{2,1,0:T(8,128)(2,1)S(1)} all-to-all(bf16[32,24,128]{2,1,0:T(8,128)(2,1)S(1)} %bitcast.9), channel_id=1, replica_groups=mesh['row'=32,'col'=32] {'col'}, dimensions={0} | all-to-all | bytes 393216 | tf_op jit(solution)/shard_map/all_to_all | solution.py:260
  99.6 0.0 copy-done.4
  99.6 1.0 s5.1
Async XLA Ops:
  0.6 24.5 %copy-start.3 = (bf16[512,512]{1,0:T(8,128)(2,1)S(1)}, bf16[512,512]{1,0:T(8,128)(2,1)}, u32[]{:S(2)}) copy-start(bf16[512,512]{1,0:T(8,128)(2,1)} %constant.16.clone.refs_1_) | copy-start | bytes 1572868
  2.1 23.0 %copy-start = (f32[256,128]{1,0:T(8,128)S(1)}, f32[256,128]{1,0:T(8,128)}, u32[]{:S(2)}) copy-start(f32[256,128]{1,0:T(8,128)} %constant.20.clone.refs_4_) | copy-start | bytes 393220
  2.1 23.0 %copy-start.1 = (f32[256,128]{1,0:T(8,128)S(1)}, f32[256,128]{1,0:T(8,128)}, u32[]{:S(2)}) copy-start(f32[256,128]{1,0:T(8,128)} %constant.19.clone.refs_3_) | copy-start | bytes 393220
  2.1 23.0 %copy-start.5 = (bf16[128,256]{1,0:T(8,128)(2,1)S(1)}, bf16[128,256]{1,0:T(8,128)(2,1)}, u32[]{:S(2)}) copy-start(bf16[128,256]{1,0:T(8,128)(2,1)} %constant.18.clone.refs_2_) | copy-start | bytes 196612
  25.2 37.6 %copy-start.6 = (bf16[256,256]{1,0:T(8,128)(2,1)S(1)}, bf16[256,256]{1,0:T(8,128)(2,1)}, u32[]{:S(2)}) copy-start(bf16[256,256]{1,0:T(8,128)(2,1)} %refs_1_.4) | copy-start | bytes 393220
  25.2 37.6 %copy-start.7 = (bf16[256,256]{1,0:T(8,128)(2,1)S(1)}, bf16[256,256]{1,0:T(8,128)(2,1)}, u32[]{:S(2)}) copy-start(bf16[256,256]{1,0:T(8,128)(2,1)} %refs_2_.4) | copy-start | bytes 393220
  25.2 37.6 %copy-start.8 = (f32[256]{0:T(256)S(1)}, f32[256]{0:T(256)}, u32[]{:S(2)}) copy-start(f32[256]{0:T(256)} %param.17) | copy-start | bytes 3076
  26.3 57.2 %copy-start.2 = (bf16[512,512]{1,0:T(8,128)(2,1)S(1)}, bf16[512,512]{1,0:T(8,128)(2,1)}, u32[]{:S(2)}) copy-start(bf16[512,512]{1,0:T(8,128)(2,1)} %constant.17.clone.refs_1_) | copy-start | bytes 1572868
  84.4 15.2 %copy-start.4 = (bf16[512,384]{1,0:T(8,128)(2,1)S(1)}, bf16[512,384]{1,0:T(8,128)(2,1)}, u32[]{:S(2)}) copy-start(bf16[512,384]{1,0:T(8,128)(2,1)} %constant.15.clone.refs_1_) | copy-start | bytes 1179652

commit v4 on v3

--- a/solution.py
+++ b/solution.py
@@ -20,6 +20,7 @@
 ITEMS = 2 * PER
 WAVES = KEEP // G
 LANES = 128
+FIRST = {"row": 23, "col": 20}
 BF = jnp.bfloat16
 F32 = jnp.float32
 
@@ -212,19 +213,29 @@
     return tuple(dot(v, table, 0, 0)[: ZL * YL].astype(BF) for v in unpack(x, roll))
 
 
-def call(fn, out, *args, fast=(True, True)):
+def turn(x, blocks):
+    n = x.shape[0] // G * blocks
+    return jnp.concatenate((x[n:], x[:n]), axis=0)
+
+
+def call(fn, out, *args, axes=(None, None)):
     outs = out if isinstance(out, list) else [out]
     single = outs is not out
 
     def kernel(*refs):
-        result = fn(*(r[...] for r in refs[: len(args)]))
+        values = [r[...] for r in refs[: len(args)]]
+        if axes[0]:
+            values[0] = turn(values[0], G - FIRST[axes[0]])
+        result = fn(*values)
+        if axes[1]:
+            result = turn(result, FIRST[axes[1]])
         for ref, value in zip(refs[len(args) :], (result,) if single else result, strict=True):
             ref[...] = value
 
     vmem = pl.BlockSpec(memory_space=pltpu.VMEM)
-    make = pltpu.VMEM if fast[1] else jax.ShapeDtypeStruct
+    make = pltpu.VMEM if axes[1] else jax.ShapeDtypeStruct
     shapes = tuple(make(s, BF) for s in outs)
-    if fast[0]:
+    if axes[0]:
         args = [pltpu.with_memory_space_constraint(a, pltpu.VMEM) for a in args]
     result = pl.pallas_call(
         kernel,
@@ -257,7 +268,9 @@
     def exchange(x, axis):
         shape = x.shape
         x = x.reshape(G, -1, shape[-1])
-        return lax.all_to_all(x, axis, split_axis=0, concat_axis=0, tiled=True).reshape(shape)
+        group = [(i + FIRST[axis]) % G for i in range(G)]
+        x = lax.all_to_all(x, axis, split_axis=0, concat_axis=0, tiled=True, axis_index_groups=[group])
+        return x.reshape(shape)
 
     def s1(*a):
         return stage1(*a, roll)
@@ -275,15 +288,15 @@
         return stage5(*a, roll)
 
     flat = (ZL * YL, NX)
-    x = call(s1, (G * 24, LANES), pressure_rhs.reshape(flat), scalar_source.reshape(flat), fwd_x, fast=(False, True))
+    x = call(s1, (G * 24, LANES), pressure_rhs.reshape(flat), scalar_source.reshape(flat), fwd_x, axes=(None, "col"))
     x = exchange(x, "col")
-    x = call(s2, (G, 4, 3 * LANES), x, outer_f, inner_f, cw, sw)
+    x = call(s2, (G, 4, 3 * LANES), x, outer_f, inner_f, cw, sw, axes=("col", "row"))
     x = exchange(x, "row")
-    x = call(s3, (G, 4, 3 * LANES), x, forward_y, back_y, wall_rates.reshape(1, NY))
+    x = call(s3, (G, 4, 3 * LANES), x, forward_y, back_y, wall_rates.reshape(1, NY), axes=("row", "row"))
     x = exchange(x, "row")
-    x = call(s4, (G * 24, LANES), x, outer_b, inner_b, cw, sw)
+    x = call(s4, (G * 24, LANES), x, outer_b, inner_b, cw, sw, axes=("row", "col"))
     x = exchange(x, "col")
-    outs = call(s5, [flat, flat], x, back_x, fast=(True, False))
+    outs = call(s5, [flat, flat], x, back_x, axes=("col", None))
     return tuple(o.reshape(ZL, YL, NX) for o in outs)
 
 

time: 101 us -> 88.7 us (0.88)
  blocking collectives: 94.8 us -> 82.6 us
    all_to_all x4, blocking collectives: 94.8 us -> 82.6 us  [exchange(): lax.all_to_all(x, axis, split_axis=0, concat_axis=0, tiled=True, axis_ind...]
where the time goes in v4:
time: 88.7 us; the launch traced here: 88.4 us
  blocking collectives  82.6 us (93%)
  Pallas kernels  5 us (6%)
    all_to_all x4, blocking collectives, exchange(): lax.all_to_all(x, axis, split_axis=0, concat_axis=0, tiled=True, axis_ind...  82.6 us
    pallas_call x5, Pallas kernels, call(): pl.pallas_call(kernel, out_shape=shapes, in_specs=[vmem] * len(args), out...  5 us

profile of v4, /device:TPU:1, one launch (start us, length us, event | category | flops | bytes accessed | tf_op | source)
XLA Modules:
  0.0 88.4 jit_solution(16902742031167415770)
XLA Ops:
  0.6 0.0 copy-start.3
  0.6 1.5 %s1_.1 = bf16[768,128]{1,0:T(8,128)(2,1)S(1)} custom-call(bf16[96,384]{1,0:T(8,128)(2,1)} %bitcast.14, bf16[96,384]{1,0:T(8,128)(2,1)} %bitcast.15, bf16[512,384]{1,0:T(8,128)(2,1)} %constant.14.clone.refs_2_), custom_call_target="tpu_custom_call" | custom-call | tf_op jit(solution)/shard_map/s1/pallas_call | solution.py:240
  2.1 0.0 copy-start
  2.1 0.0 copy-start.1
  2.1 0.0 copy-start.5
  2.1 17.7 %all_to_all.20 = bf16[32,24,128]{2,1,0:T(8,128)(2,1)S(1)} all-to-all(bf16[32,24,128]{2,1,0:T(8,128)(2,1)S(1)} %bitcast.12), channel_id=1, replica_groups={{20,21,22,23,24,25,26,27,28,29,30,31,0,1,2,3,4,5,6,7,8,9,10,11,12,13,14..., dimensions={0} | all-to-all | bytes 393216 | tf_op jit(solution)/shard_map/all_to_all | solution.py:272
  19.8 0.0 copy-done.3
  19.8 0.0 copy-done
  19.8 0.0 copy-done.1
  19.8 0.0 copy-done.5
  19.8 0.0 copy-start.6
  19.8 0.0 copy-start.7
  19.8 0.0 copy-start.8
  19.8 1.1 %s2_.1 = bf16[32,4,384]{2,1,0:T(4,128)(2,1)S(1)} custom-call(bf16[768,128]{1,0:T(8,128)(2,1)S(1)} %bitcast.10, bf16[512,512]{1,0:T(8,128)(2,1)S(1)} %copy-done.3, bf16[128,256]{1,0:T(8,128)(2,1)S(1)} %copy-done.5, f32[256,128]{1,0:T(8,128)S(1)} %copy-done.1, f32[256,128]{1,0:T(8,128)S(1)} %copy-done), custom_call_target="tpu_custom_call" | custom-call | tf_op jit(solution)/shard_map/s2/pallas_call | solution.py:240
  20.9 0.0 copy-start.2
  20.9 30.8 %all_to_all.21.refs_0_ = bf16[32,4,384]{2,1,0:T(4,128)(2,1)S(1)} all-to-all(bf16[32,4,384]{2,1,0:T(4,128)(2,1)S(1)} %s2_.1), channel_id=1, replica_groups={{736,768,800,832,864,896,928,960,992,0,32,64,96,128,160,192,224,256,288..., dimensions={0} | all-to-all | bytes 196608 | tf_op jit(solution)/shard_map/all_to_all | solution.py:272
  51.7 0.0 copy-done.6
  51.7 0.0 copy-done.7
  51.7 0.0 copy-done.8
  51.7 0.5 s3.1
  52.2 19.4 %all_to_all.22.refs_0_ = bf16[32,4,384]{2,1,0:T(4,128)(2,1)S(1)} all-to-all(bf16[32,4,384]{2,1,0:T(4,128)(2,1)S(1)} %s3.1), channel_id=1, replica_groups={{736,768,800,832,864,896,928,960,992,0,32,64,96,128,160,192,224,256,288..., dimensions={0} | all-to-all | bytes 196608 | tf_op jit(solution)/shard_map/all_to_all | solution.py:272
  71.6 0.0 copy-done.2
  71.6 1.0 %s4_.1 = bf16[768,128]{1,0:T(8,128)(2,1)S(1)} custom-call(bf16[32,4,384]{2,1,0:T(4,128)(2,1)S(1)} %all_to_all.22.refs_0_, bf16[512,512]{1,0:T(8,128)(2,1)S(1)} %copy-done.2, bf16[128,256]{1,0:T(8,128)(2,1)S(1)} %copy-done.5, f32[256,128]{1,0:T(8,128)S(1)} %copy-done.1, f32[256,128]{1,0:T(8,128)S(1)} %copy-done), custom_call_target="tpu_custom_call" | custom-call | tf_op jit(solution)/shard_map/s4/pallas_call | solution.py:240
  72.6 0.0 copy-start.4
  72.6 14.8 %all_to_all.23 = bf16[32,24,128]{2,1,0:T(8,128)(2,1)S(1)} all-to-all(bf16[32,24,128]{2,1,0:T(8,128)(2,1)S(1)} %bitcast.9), channel_id=1, replica_groups={{20,21,22,23,24,25,26,27,28,29,30,31,0,1,2,3,4,5,6,7,8,9,10,11,12,13,14..., dimensions={0} | all-to-all | bytes 393216 | tf_op jit(solution)/shard_map/all_to_all | solution.py:272
  87.4 0.0 copy-done.4
  87.4 1.0 %s5.1 = (bf16[96,384]{1,0:T(8,128)(2,1)}, bf16[96,384]{1,0:T(8,128)(2,1)}) custom-call(bf16[768,128]{1,0:T(8,128)(2,1)S(1)} %bitcast.11, bf16[512,384]{1,0:T(8,128)(2,1)S(1)} %copy-done.4), custom_call_target="tpu_custom_call" | custom-call | tf_op jit(solution)/shard_map/s5/pallas_call | solution.py:240
Async XLA Ops:
  0.6 19.2 %copy-start.3 = (bf16[512,512]{1,0:T(8,128)(2,1)S(1)}, bf16[512,512]{1,0:T(8,128)(2,1)}, u32[]{:S(2)}) copy-start(bf16[512,512]{1,0:T(8,128)(2,1)} %constant.16.clone.refs_1_) | copy-start | bytes 1572868
  2.1 17.7 %copy-start = (f32[256,128]{1,0:T(8,128)S(1)}, f32[256,128]{1,0:T(8,128)}, u32[]{:S(2)}) copy-start(f32[256,128]{1,0:T(8,128)} %constant.20.clone.refs_4_) | copy-start | bytes 393220
  2.1 17.7 %copy-start.1 = (f32[256,128]{1,0:T(8,128)S(1)}, f32[256,128]{1,0:T(8,128)}, u32[]{:S(2)}) copy-start(f32[256,128]{1,0:T(8,128)} %constant.19.clone.refs_3_) | copy-start | bytes 393220
  2.1 17.7 %copy-start.5 = (bf16[128,256]{1,0:T(8,128)(2,1)S(1)}, bf16[128,256]{1,0:T(8,128)(2,1)}, u32[]{:S(2)}) copy-start(bf16[128,256]{1,0:T(8,128)(2,1)} %constant.18.clone.refs_2_) | copy-start | bytes 196612
  19.8 31.9 %copy-start.6 = (bf16[256,256]{1,0:T(8,128)(2,1)S(1)}, bf16[256,256]{1,0:T(8,128)(2,1)}, u32[]{:S(2)}) copy-start(bf16[256,256]{1,0:T(8,128)(2,1)} %refs_1_.4) | copy-start | bytes 393220
  19.8 31.9 %copy-start.7 = (bf16[256,256]{1,0:T(8,128)(2,1)S(1)}, bf16[256,256]{1,0:T(8,128)(2,1)}, u32[]{:S(2)}) copy-start(bf16[256,256]{1,0:T(8,128)(2,1)} %refs_2_.4) | copy-start | bytes 393220
  19.8 31.8 %copy-start.8 = (f32[256]{0:T(256)S(1)}, f32[256]{0:T(256)}, u32[]{:S(2)}) copy-start(f32[256]{0:T(256)} %param.17) | copy-start | bytes 3076
  20.9 50.7 %copy-start.2 = (bf16[512,512]{1,0:T(8,128)(2,1)S(1)}, bf16[512,512]{1,0:T(8,128)(2,1)}, u32[]{:S(2)}) copy-start(bf16[512,512]{1,0:T(8,128)(2,1)} %constant.17.clone.refs_1_) | copy-start | bytes 1572868
  72.6 14.8 %copy-start.4 = (bf16[512,384]{1,0:T(8,128)(2,1)S(1)}, bf16[512,384]{1,0:T(8,128)(2,1)}, u32[]{:S(2)}) copy-start(bf16[512,384]{1,0:T(8,128)(2,1)} %constant.15.clone.refs_1_) | copy-start | bytes 1179652

commit v5 on v4

--- a/solution.py
+++ b/solution.py
@@ -19,6 +19,7 @@
 PER = NX // 2 // G
 ITEMS = 2 * PER
 WAVES = KEEP // G
+LINE = G * PER
 LANES = 128
 FIRST = {"row": 23, "col": 20}
 BF = jnp.bfloat16
@@ -52,14 +53,6 @@
     return fwd.reshape(-1, NX), back.reshape(-1, NX)
 
 
-def waves(table, axis):
-    shape = list(table.shape)
-    shape[axis : axis + 2] = [2, G // 2 * PER]
-    pad = [(0, 0)] * len(shape)
-    pad[axis + 1] = (0, LANES - shape[axis + 1])
-    return np.pad(table.reshape(shape), pad)
-
-
 def z_outer(sign):
     out = np.zeros((2, G, PER, 2, G, 8))
     angle = 2.0 * math.pi * (np.outer(np.arange(G), np.arange(G)) % G) / G
@@ -67,7 +60,7 @@
     for h, i, p, k in items():
         for q in range(2):
             out[q, :, k, h, :, i] = pairs(q, p, cos, sin, sign)
-    return waves(out, 1).reshape(4 * LANES, 2 * G * 8)
+    return out.reshape(2 * LINE, 2 * G * 8)
 
 
 def z_outer_back():
@@ -77,7 +70,7 @@
     for h, i, p, k in items():
         for q in range(2):
             out[h, :, i, q, :, k] = pairs(p, q, cos, sin, 1)
-    return waves(out, 4).reshape(2 * G * 8, 4 * LANES)
+    return out.reshape(2 * G * 8, 2 * LINE)
 
 
 def z_inner(sign):
@@ -94,8 +87,8 @@
 
 def twiddles():
     angle = 2.0 * math.pi * np.outer(np.arange(G), np.arange(ZL)) / NZ
-    angle = np.repeat(np.repeat(angle, PER, axis=0).reshape(G, PER, ZL), YL, axis=2)
-    angle = np.pad(waves(angle, 0).reshape(2 * LANES, ZL * YL), ((0, 0), (0, LANES - ZL * YL)))
+    angle = np.repeat(np.repeat(angle, PER, axis=0), YL, axis=1)
+    angle = np.pad(angle, ((0, 0), (0, LANES - ZL * YL)))
     return np.cos(angle), np.sin(angle)
 
 
@@ -120,45 +113,19 @@
     )
 
 
-def swap_blocks(rows, roll):
-    lane = lax.broadcasted_iota(jnp.int32, (8, LANES), 1) // PER
-    x = list(rows)
-    for d in (8, 4, 2, 1):
-        high = (lane & d) != 0
-        for i in range(16):
-            if not i & d:
-                a, b = x[i], x[i + d]
-                x[i] = jnp.where(high, roll(b, PER * d, 1), a)
-                x[i + d] = jnp.where(high, b, roll(a, LANES - PER * d, 1))
-    return x
-
-
-def fold(z, roll):
-    lane = lax.broadcasted_iota(jnp.int32, (NY, LANES), 1)
-    moved = roll(z[1], LANES - LANES // 4, 1)
-    whole = jnp.where(lane < 3 * LANES // 4, z[0], moved).reshape(G, YL, LANES)
-    low = moved.reshape(G, YL, LANES)[:, :4]
-    high = roll(moved, LANES // 2, 1).reshape(G, YL, LANES)[:, 4:]
-    lane = lax.broadcasted_iota(jnp.int32, (G, 4, LANES), 2)
-    rest = jnp.where(lane < LANES // 2, low, high)
-    return jnp.concatenate((whole[:, :4], whole[:, 4:], rest), axis=2).astype(BF)
-
-
-def unfold(x, roll):
+def fold(x):
+    x = x.reshape(G, YL, LINE)
+    low, high = x[:, :4], x[:, 4:]
+    parts = (low[:, :, :LANES], high[:, :, :LANES], low[:, :, LANES:], high[:, :, LANES:])
+    return jnp.concatenate(parts, axis=2).astype(BF)
+
+
+def unfold(x):
     x = x.astype(F32)
-    rest = x[:, :, 2 * LANES :]
-    whole = jnp.concatenate((x[:, :, :LANES], x[:, :, LANES : 2 * LANES]), axis=1).reshape(NY, LANES)
-    rest = jnp.concatenate((rest, roll(rest, LANES // 2, 2)), axis=1).reshape(NY, LANES)
-    return whole, rest
-
-
-def refold(whole, rest, roll):
-    lane = lax.broadcasted_iota(jnp.int32, (G, 4, LANES), 2)
-    low = rest.reshape(G, YL, LANES)[:, :4]
-    high = roll(rest, LANES // 2, 1).reshape(G, YL, LANES)[:, 4:]
-    whole = whole.reshape(G, YL, LANES)
-    rest = jnp.where(lane < LANES // 2, low, high)
-    return jnp.concatenate((whole[:, :4], whole[:, 4:], rest), axis=2).astype(BF)
+    half = LANES // 2
+    low = jnp.concatenate((x[:, :, :LANES], x[:, :, 2 * LANES : 2 * LANES + half]), axis=2)
+    high = jnp.concatenate((x[:, :, LANES : 2 * LANES], x[:, :, 2 * LANES + half :]), axis=2)
+    return jnp.concatenate((low, high), axis=1).reshape(NY, LINE).astype(BF)
 
 
 def stage1(p, s, table, roll):
@@ -168,41 +135,28 @@
 
 
 def stage2(x, outer, inner, cw, sw, roll):
-    n = G * 8
+    n = LINE
     g = dot(outer, jnp.concatenate(unpack(x, roll), axis=1))
-    cols = []
+    parts = []
     for f in range(2):
         re, im = (g[j * n : (j + 1) * n, f * LANES : (f + 1) * LANES] for j in range(2))
         h = jnp.concatenate((re * cw + im * sw, im * cw - re * sw), axis=1).astype(BF)
-        o = dot(inner, h, 1, 1)
-        rows = []
-        for q in range(2):
-            rows += swap_blocks([o[8 * i : 8 * i + 8, q * LANES : (q + 1) * LANES] for i in range(16)], roll)
-        cols.append(jnp.concatenate(rows, axis=0))
-    return fold(cols, roll)
-
-
-def stage3(x, forward_y, back_y, wall, row_at, col_at, roll):
-    wall = jnp.broadcast_to(wall, (LANES, NY)).T
-    lane = lax.broadcasted_iota(jnp.int32, (1, LANES), 1)
-    c = dot(forward_y, jnp.concatenate(unfold(x, roll), axis=1).astype(BF))
-    total = wall + wave_numbers(jnp.where(lane < 96, lane, lane - 96), row_at, col_at)
-    scale = jnp.where(lane < 96, -total, 1.0 + DIFFUSION * total)
-    rest = 1.0 + DIFFUSION * (wall + wave_numbers(lane % 64 + 32, row_at, col_at))
-    hat = jnp.concatenate((c[:, :LANES] / scale, c[:, LANES:] / rest), axis=1).astype(BF)
-    e = dot(back_y, hat)
-    return refold(e[:, :LANES], e[:, LANES:], roll)
+        parts.append(dot(inner, h, 1, 1))
+    return fold(jnp.concatenate(parts, axis=0))
+
+
+def stage3(x, forward_y, back_y, wall, row_at, col_at):
+    c = dot(forward_y, unfold(x))
+    total = jnp.broadcast_to(wall, (LINE, NY)).T + wave_numbers(row_at, col_at)
+    hat = c / jnp.where(row_at < G // 2, -total, 1.0 + DIFFUSION * total)
+    return fold(dot(back_y, hat.astype(BF)))
 
 
 def stage4(x, outer, inner, cw, sw, roll):
-    whole, rest = unfold(x, roll)
-    lane = lax.broadcasted_iota(jnp.int32, (NY, LANES), 1)
-    second = jnp.where(lane < LANES // 4, roll(whole, LANES // 4, 1), roll(rest, LANES // 4, 1))
+    z = unfold(x)
     parts = []
-    for z in (whole, second):
-        tiles = [z[8 * r : 8 * r + 8] for r in range(G)]
-        halves = [jnp.concatenate(swap_blocks(tiles[16 * q : 16 * q + 16], roll), axis=0) for q in range(2)]
-        v = jnp.concatenate(halves, axis=1).astype(BF)
+    for f in range(2):
+        v = z[f * LANES : (f + 1) * LANES]
         h = dot(v, inner, 0, 0)
         re, im = h[:, :LANES], h[:, LANES:]
         parts.append(jnp.concatenate((re * cw - im * sw, im * cw + re * sw), axis=0).astype(BF))
@@ -247,11 +201,11 @@
     return result[0] if single else result
 
 
-def wave_numbers(lane, row_at, col_at):
-    k = lane % PER
-    t = lane // PER % WAVES
-    m = col_at * PER + k
-    n = row_at + G * t
+def wave_numbers(row_at, col_at):
+    item = lax.broadcasted_iota(jnp.int32, (1, LINE), 1)
+    t = row_at % WAVES
+    m = col_at * PER + item % PER
+    n = item // PER + G * t
     signed = jnp.where(t < WAVES // 2, n, n - KEEP)
     kx_sq = (m.astype(F32) * (2.0 * math.pi / NX)) ** 2
     kz_sq = (signed.astype(F32) * (2.0 * math.pi / NZ)) ** 2
@@ -279,7 +233,7 @@
         return stage2(*a, roll)
 
     def s3(*a):
-        return stage3(*a, lax.axis_index("row"), lax.axis_index("col"), roll)
+        return stage3(*a, lax.axis_index("row"), lax.axis_index("col"))
 
     def s4(*a):
         return stage4(*a, roll)

time: 88.7 us -> 87.8 us (0.990)
  Pallas kernels: 5 us -> 4.08 us
    pallas_call x5, Pallas kernels: 5 us -> 4.08 us  [call(): pl.pallas_call(kernel, out_shape=shapes, in_specs=[vmem] * len(args), out...]
where the time goes in v5:
time: 87.8 us; the launch traced here: 87.4 us
  blocking collectives  82.6 us (94%)
  Pallas kernels  4.08 us (5%)
    all_to_all x4, blocking collectives, exchange(): lax.all_to_all(x, axis, split_axis=0, concat_axis=0, tiled=True, axis_ind...  82.6 us
    pallas_call x5, Pallas kernels, call(): pl.pallas_call(kernel, out_shape=shapes, in_specs=[vmem] * len(args), out...  4.08 us

profile of v5, /device:TPU:1, one launch (start us, length us, event | category | flops | bytes accessed | tf_op | source)
XLA Modules:
  0.0 87.4 jit_solution(18168997916864374029)
XLA Ops:
  0.6 0.0 copy-start.4
  0.6 1.4 %s1_.1 = bf16[768,128]{1,0:T(8,128)(2,1)S(1)} custom-call(bf16[96,384]{1,0:T(8,128)(2,1)} %bitcast.14, bf16[96,384]{1,0:T(8,128)(2,1)} %bitcast.15, bf16[512,384]{1,0:T(8,128)(2,1)} %constant.14.clone.refs_2_), custom_call_target="tpu_custom_call" | custom-call | tf_op jit(solution)/shard_map/s1/pallas_call | solution.py:194
  2.1 0.0 copy-start
  2.1 0.0 copy-start.1
  2.1 0.0 copy-start.5
  2.1 17.7 %all_to_all.20 = bf16[32,24,128]{2,1,0:T(8,128)(2,1)S(1)} all-to-all(bf16[32,24,128]{2,1,0:T(8,128)(2,1)S(1)} %bitcast.10), channel_id=1, replica_groups={{20,21,22,23,24,25,26,27,28,29,30,31,0,1,2,3,4,5,6,7,8,9,10,11,12,13,14..., dimensions={0} | all-to-all | bytes 393216 | tf_op jit(solution)/shard_map/all_to_all | solution.py:226
  19.8 0.0 copy-done.4
  19.8 0.0 copy-done
  19.8 0.0 copy-done.1
  19.8 0.0 copy-done.5
  19.8 0.0 copy-start.6
  19.8 0.0 copy-start.7
  19.8 0.0 copy-start.8
  19.8 0.6 s2_.1
  20.4 0.0 copy-start.3
  20.4 30.8 %all_to_all.21.refs_0_ = bf16[32,4,384]{2,1,0:T(4,128)(2,1)S(1)} all-to-all(bf16[32,4,384]{2,1,0:T(4,128)(2,1)S(1)} %s2_.1), channel_id=1, replica_groups={{736,768,800,832,864,896,928,960,992,0,32,64,96,128,160,192,224,256,288..., dimensions={0} | all-to-all | bytes 196608 | tf_op jit(solution)/shard_map/all_to_all | solution.py:226
  51.2 0.0 copy-done.6
  51.2 0.0 copy-done.7
  51.2 0.0 copy-done.8
  51.2 0.5 s3.1
  51.8 19.4 %all_to_all.22.refs_0_ = bf16[32,4,384]{2,1,0:T(4,128)(2,1)S(1)} all-to-all(bf16[32,4,384]{2,1,0:T(4,128)(2,1)S(1)} %s3.1), channel_id=1, replica_groups={{736,768,800,832,864,896,928,960,992,0,32,64,96,128,160,192,224,256,288..., dimensions={0} | all-to-all | bytes 196608 | tf_op jit(solution)/shard_map/all_to_all | solution.py:226
  71.1 0.0 copy-done.3
  71.1 0.5 s4_.1
  71.7 0.0 copy-start.2
  71.7 14.8 %all_to_all.23 = bf16[32,24,128]{2,1,0:T(8,128)(2,1)S(1)} all-to-all(bf16[32,24,128]{2,1,0:T(8,128)(2,1)S(1)} %bitcast.11), channel_id=1, replica_groups={{20,21,22,23,24,25,26,27,28,29,30,31,0,1,2,3,4,5,6,7,8,9,10,11,12,13,14..., dimensions={0} | all-to-all | bytes 393216 | tf_op jit(solution)/shard_map/all_to_all | solution.py:226
  86.5 0.0 copy-done.2
  86.5 1.0 %s5.1 = (bf16[96,384]{1,0:T(8,128)(2,1)}, bf16[96,384]{1,0:T(8,128)(2,1)}) custom-call(bf16[768,128]{1,0:T(8,128)(2,1)S(1)} %bitcast.9, bf16[512,384]{1,0:T(8,128)(2,1)S(1)} %copy-done.2), custom_call_target="tpu_custom_call" | custom-call | tf_op jit(solution)/shard_map/s5/pallas_call | solution.py:194
Async XLA Ops:
  0.6 19.2 %copy-start.4 = (bf16[384,512]{1,0:T(8,128)(2,1)S(1)}, bf16[384,512]{1,0:T(8,128)(2,1)}, u32[]{:S(2)}) copy-start(bf16[384,512]{1,0:T(8,128)(2,1)} %constant.16.clone.refs_1_) | copy-start | bytes 1179652
  2.1 17.7 %copy-start = (f32[192,128]{1,0:T(8,128)S(1)}, f32[192,128]{1,0:T(8,128)}, u32[]{:S(2)}) copy-start(f32[192,128]{1,0:T(8,128)} %constant.20.clone.refs_4_) | copy-start | bytes 294916
  2.1 17.7 %copy-start.1 = (f32[192,128]{1,0:T(8,128)S(1)}, f32[192,128]{1,0:T(8,128)}, u32[]{:S(2)}) copy-start(f32[192,128]{1,0:T(8,128)} %constant.19.clone.refs_3_) | copy-start | bytes 294916
  2.1 17.7 %copy-start.5 = (bf16[128,256]{1,0:T(8,128)(2,1)S(1)}, bf16[128,256]{1,0:T(8,128)(2,1)}, u32[]{:S(2)}) copy-start(bf16[128,256]{1,0:T(8,128)(2,1)} %constant.18.clone.refs_2_) | copy-start | bytes 196612
  19.8 31.4 %copy-start.6 = (bf16[256,256]{1,0:T(8,128)(2,1)S(1)}, bf16[256,256]{1,0:T(8,128)(2,1)}, u32[]{:S(2)}) copy-start(bf16[256,256]{1,0:T(8,128)(2,1)} %refs_1_.4) | copy-start | bytes 393220
  19.8 31.4 %copy-start.7 = (bf16[256,256]{1,0:T(8,128)(2,1)S(1)}, bf16[256,256]{1,0:T(8,128)(2,1)}, u32[]{:S(2)}) copy-start(bf16[256,256]{1,0:T(8,128)(2,1)} %refs_2_.4) | copy-start | bytes 393220
  19.8 31.4 %copy-start.8 = (f32[256]{0:T(256)S(1)}, f32[256]{0:T(256)}, u32[]{:S(2)}) copy-start(f32[256]{0:T(256)} %param.17) | copy-start | bytes 3076
  20.4 50.7 %copy-start.3 = (bf16[512,384]{1,0:T(8,128)(2,1)S(1)}, bf16[512,384]{1,0:T(8,128)(2,1)}, u32[]{:S(2)}) copy-start(bf16[512,384]{1,0:T(8,128)(2,1)} %constant.17.clone.refs_1_) | copy-start | bytes 1179652
  71.7 14.8 %copy-start.2 = (bf16[512,384]{1,0:T(8,128)(2,1)S(1)}, bf16[512,384]{1,0:T(8,128)(2,1)}, u32[]{:S(2)}) copy-start(bf16[512,384]{1,0:T(8,128)(2,1)} %constant.15.clone.refs_1_) | copy-start | bytes 1179652

commit v6 on v5

--- a/solution.py
+++ b/solution.py
@@ -21,7 +21,7 @@
 WAVES = KEEP // G
 LINE = G * PER
 LANES = 128
-FIRST = {"row": 23, "col": 20}
+ORDER = {"row": [(23 + i) % G for i in range(G)], "col": [(20 + i) % G for i in range(G)]}
 BF = jnp.bfloat16
 F32 = jnp.float32
 
@@ -96,17 +96,36 @@
     return lax.dot_general(a, b, (((ca,), (cb,)), ((), ())), preferred_element_type=F32)
 
 
+def send(x, axis):
+    return jnp.concatenate([x[i : i + 1] for i in ORDER[axis]], axis=0)
+
+
+def receive(x, axis):
+    place = [ORDER[axis].index(i) for i in range(G)]
+    return jnp.concatenate([x[i : i + 1] for i in place], axis=0)
+
+
 def pack(g, roll):
     n = G * 8
     mid = g[n:, :LANES] + roll(g[n:, LANES:], 4, 0)
-    tiles = [v.reshape(G, 8, LANES) for v in (g[:n, :LANES], mid, g[:n, LANES:])]
-    return jnp.concatenate(tiles, axis=1).reshape(G * 24, LANES).astype(BF)
+    lane = lax.broadcasted_iota(jnp.int32, (n, LANES), 1)
+    one, two = (roll(g[:n, LANES:], shift, 1) for shift in (96, 64))
+    first = jnp.where(lane < 96, g[:n, :LANES], one).reshape(G, 2, 4, LANES)
+    mid = jnp.where(lane < 96, mid, two).reshape(G, 2, 4, LANES)
+    lane = lax.broadcasted_iota(jnp.int32, (G, 4, LANES), 2)
+    low, high = two.reshape(G, 8, LANES)[:, :4], one.reshape(G, 8, LANES)[:, 4:]
+    rest = jnp.where(lane < 32, low, high).reshape(G, 1, 4, LANES)
+    return send(jnp.concatenate((first, mid, rest), axis=1), "col").astype(BF)
 
 
 def unpack(x, roll):
     n = G * 8
-    x = x.astype(F32).reshape(G, 24, LANES)
-    first, mid, last = (x[:, 8 * j : 8 * j + 8].reshape(n, LANES) for j in range(3))
+    x = receive(x.astype(F32), "col")
+    first, mid = x[:, :2].reshape(n, LANES), x[:, 2:4].reshape(n, LANES)
+    rest = jnp.concatenate((x[:, 4], roll(x[:, 4], 96, 2)), axis=1).reshape(n, LANES)
+    lane = lax.broadcasted_iota(jnp.int32, (n, LANES), 1)
+    last = roll(jnp.where(lane < 32, rest, mid), 64, 1)
+    last = jnp.where(lane < 32, roll(first, 32, 1), last)
     return (
         jnp.concatenate((first, mid), axis=0).astype(BF),
         jnp.concatenate((last, roll(mid, n - 4, 0)), axis=0).astype(BF),
@@ -117,11 +136,11 @@
     x = x.reshape(G, YL, LINE)
     low, high = x[:, :4], x[:, 4:]
     parts = (low[:, :, :LANES], high[:, :, :LANES], low[:, :, LANES:], high[:, :, LANES:])
-    return jnp.concatenate(parts, axis=2).astype(BF)
+    return send(jnp.concatenate(parts, axis=2), "row").astype(BF)
 
 
 def unfold(x):
-    x = x.astype(F32)
+    x = receive(x.astype(F32), "row")
     half = LANES // 2
     low = jnp.concatenate((x[:, :, :LANES], x[:, :, 2 * LANES : 2 * LANES + half]), axis=2)
     high = jnp.concatenate((x[:, :, LANES : 2 * LANES], x[:, :, 2 * LANES + half :]), axis=2)
@@ -167,29 +186,19 @@
     return tuple(dot(v, table, 0, 0)[: ZL * YL].astype(BF) for v in unpack(x, roll))
 
 
-def turn(x, blocks):
-    n = x.shape[0] // G * blocks
-    return jnp.concatenate((x[n:], x[:n]), axis=0)
-
-
-def call(fn, out, *args, axes=(None, None)):
+def call(fn, out, *args, fast=(True, True)):
     outs = out if isinstance(out, list) else [out]
     single = outs is not out
 
     def kernel(*refs):
-        values = [r[...] for r in refs[: len(args)]]
-        if axes[0]:
-            values[0] = turn(values[0], G - FIRST[axes[0]])
-        result = fn(*values)
-        if axes[1]:
-            result = turn(result, FIRST[axes[1]])
+        result = fn(*(r[...] for r in refs[: len(args)]))
         for ref, value in zip(refs[len(args) :], (result,) if single else result, strict=True):
             ref[...] = value
 
     vmem = pl.BlockSpec(memory_space=pltpu.VMEM)
-    make = pltpu.VMEM if axes[1] else jax.ShapeDtypeStruct
+    make = pltpu.VMEM if fast[1] else jax.ShapeDtypeStruct
     shapes = tuple(make(s, BF) for s in outs)
-    if axes[0]:
+    if fast[0]:
         args = [pltpu.with_memory_space_constraint(a, pltpu.VMEM) for a in args]
     result = pl.pallas_call(
         kernel,
@@ -220,11 +229,7 @@
     roll = pltpu.roll
 
     def exchange(x, axis):
-        shape = x.shape
-        x = x.reshape(G, -1, shape[-1])
-        group = [(i + FIRST[axis]) % G for i in range(G)]
-        x = lax.all_to_all(x, axis, split_axis=0, concat_axis=0, tiled=True, axis_index_groups=[group])
-        return x.reshape(shape)
+        return lax.all_to_all(x, axis, split_axis=0, concat_axis=0, tiled=True, axis_index_groups=[ORDER[axis]])
 
     def s1(*a):
         return stage1(*a, roll)
@@ -242,15 +247,15 @@
         return stage5(*a, roll)
 
     flat = (ZL * YL, NX)
-    x = call(s1, (G * 24, LANES), pressure_rhs.reshape(flat), scalar_source.reshape(flat), fwd_x, axes=(None, "col"))
+    x = call(s1, (G, 5, 4, LANES), pressure_rhs.reshape(flat), scalar_source.reshape(flat), fwd_x, fast=(False, True))
     x = exchange(x, "col")
-    x = call(s2, (G, 4, 3 * LANES), x, outer_f, inner_f, cw, sw, axes=("col", "row"))
+    x = call(s2, (G, 4, 3 * LANES), x, outer_f, inner_f, cw, sw)
     x = exchange(x, "row")
-    x = call(s3, (G, 4, 3 * LANES), x, forward_y, back_y, wall_rates.reshape(1, NY), axes=("row", "row"))
+    x = call(s3, (G, 4, 3 * LANES), x, forward_y, back_y, wall_rates.reshape(1, NY))
     x = exchange(x, "row")
-    x = call(s4, (G * 24, LANES), x, outer_b, inner_b, cw, sw, axes=("row", "col"))
+    x = call(s4, (G, 5, 4, LANES), x, outer_b, inner_b, cw, sw)
     x = exchange(x, "col")
-    outs = call(s5, [flat, flat], x, back_x, axes=("col", None))
+    outs = call(s5, [flat, flat], x, back_x, fast=(True, False))
     return tuple(o.reshape(ZL, YL, NX) for o in outs)
 
 

time: 87.8 us -> 86.7 us (0.987)
  blocking collectives: 82.6 us -> 81.2 us
    all_to_all x4, blocking collectives: 82.6 us -> 81.2 us  [exchange(): lax.all_to_all(x, axis, split_axis=0, concat_axis=0, tiled=True, axis_ind...]
where the time goes in v6:
time: 86.7 us; the launch traced here: 86.4 us
  blocking collectives  81.2 us (94%)
  Pallas kernels  4.37 us (5%)
    all_to_all x4, blocking collectives, exchange(): lax.all_to_all(x, axis, split_axis=0, concat_axis=0, tiled=True, axis_ind...  81.2 us
    pallas_call x5, Pallas kernels, call(): pl.pallas_call(kernel, out_shape=shapes, in_specs=[vmem] * len(args), out...  4.37 us

profile of v6, /device:TPU:1, one launch (start us, length us, event | category | flops | bytes accessed | tf_op | source)
XLA Modules:
  0.0 86.4 jit_solution(17244911809821056013)
XLA Ops:
  0.6 0.0 copy-start.1
  0.6 1.4 %s1_.1 = bf16[32,5,4,128]{3,2,1,0:T(4,128)(2,1)S(1)} custom-call(bf16[96,384]{1,0:T(8,128)(2,1)} %bitcast.6, bf16[96,384]{1,0:T(8,128)(2,1)} %bitcast.7, bf16[512,384]{1,0:T(8,128)(2,1)} %constant.14.clone.refs_2_), custom_call_target="tpu_custom_call" | custom-call | tf_op jit(solution)/shard_map/s1/pallas_call | solution.py:203
  2.1 0.0 copy-start.2
  2.1 0.0 copy-start.3
  2.1 0.0 copy-start.5
  2.1 17.4 %all_to_all.20.refs_0_ = bf16[32,5,4,128]{3,2,1,0:T(4,128)(2,1)S(1)} all-to-all(bf16[32,5,4,128]{3,2,1,0:T(4,128)(2,1)S(1)} %s1_.1), channel_id=1, replica_groups={{20,21,22,23,24,25,26,27,28,29,30,31,0,1,2,3,4,5,6,7,8,9,10,11,12,13,14..., dimensions={0} | all-to-all | bytes 327680 | tf_op jit(solution)/shard_map/all_to_all | solution.py:232
  19.5 0.0 copy-done.1
  19.5 0.0 copy-done.2
  19.5 0.0 copy-done.3
  19.5 0.0 copy-done.5
  19.5 0.0 copy-start.6
  19.5 0.0 copy-start.7
  19.6 0.0 copy-start.8
  19.6 0.7 s2_.1
  20.3 0.0 copy-start
  20.3 30.5 %all_to_all.21.refs_0_ = bf16[32,4,384]{2,1,0:T(4,128)(2,1)S(1)} all-to-all(bf16[32,4,384]{2,1,0:T(4,128)(2,1)S(1)} %s2_.1), channel_id=1, replica_groups={{736,768,800,832,864,896,928,960,992,0,32,64,96,128,160,192,224,256,288..., dimensions={0} | all-to-all | bytes 196608 | tf_op jit(solution)/shard_map/all_to_all | solution.py:232
  50.8 0.0 copy-done.6
  50.8 0.0 copy-done.7
  50.8 0.0 copy-done.8
  50.8 0.5 s3.1
  51.3 19.4 %all_to_all.22.refs_0_ = bf16[32,4,384]{2,1,0:T(4,128)(2,1)S(1)} all-to-all(bf16[32,4,384]{2,1,0:T(4,128)(2,1)S(1)} %s3.1), channel_id=1, replica_groups={{736,768,800,832,864,896,928,960,992,0,32,64,96,128,160,192,224,256,288..., dimensions={0} | all-to-all | bytes 196608 | tf_op jit(solution)/shard_map/all_to_all | solution.py:232
  70.7 0.0 copy-done
  70.7 0.0 copy-start.4
  70.7 0.6 s4_.1
  71.3 14.0 %all_to_all.23.refs_0_ = bf16[32,5,4,128]{3,2,1,0:T(4,128)(2,1)S(1)} all-to-all(bf16[32,5,4,128]{3,2,1,0:T(4,128)(2,1)S(1)} %s4_.1), channel_id=1, replica_groups={{20,21,22,23,24,25,26,27,28,29,30,31,0,1,2,3,4,5,6,7,8,9,10,11,12,13,14..., dimensions={0} | all-to-all | bytes 327680 | tf_op jit(solution)/shard_map/all_to_all | solution.py:232
  85.3 0.0 copy-done.4
  85.3 1.1 %s5.1 = (bf16[96,384]{1,0:T(8,128)(2,1)}, bf16[96,384]{1,0:T(8,128)(2,1)}) custom-call(bf16[32,5,4,128]{3,2,1,0:T(4,128)(2,1)S(1)} %all_to_all.23.refs_0_, bf16[512,384]{1,0:T(8,128)(2,1)S(1)} %copy-done.4), custom_call_target="tpu_custom_call" | custom-call | tf_op jit(solution)/shard_map/s5/pallas_call | solution.py:203
Async XLA Ops:
  0.6 18.9 %copy-start.1 = (bf16[384,512]{1,0:T(8,128)(2,1)S(1)}, bf16[384,512]{1,0:T(8,128)(2,1)}, u32[]{:S(2)}) copy-start(bf16[384,512]{1,0:T(8,128)(2,1)} %constant.16.clone.refs_1_) | copy-start | bytes 1179652
  2.1 17.4 %copy-start.2 = (f32[192,128]{1,0:T(8,128)S(1)}, f32[192,128]{1,0:T(8,128)}, u32[]{:S(2)}) copy-start(f32[192,128]{1,0:T(8,128)} %constant.20.clone.refs_4_) | copy-start | bytes 294916
  2.1 17.4 %copy-start.3 = (f32[192,128]{1,0:T(8,128)S(1)}, f32[192,128]{1,0:T(8,128)}, u32[]{:S(2)}) copy-start(f32[192,128]{1,0:T(8,128)} %constant.19.clone.refs_3_) | copy-start | bytes 294916
  2.1 17.4 %copy-start.5 = (bf16[128,256]{1,0:T(8,128)(2,1)S(1)}, bf16[128,256]{1,0:T(8,128)(2,1)}, u32[]{:S(2)}) copy-start(bf16[128,256]{1,0:T(8,128)(2,1)} %constant.18.clone.refs_2_) | copy-start | bytes 196612
  19.5 31.3 %copy-start.6 = (bf16[256,256]{1,0:T(8,128)(2,1)S(1)}, bf16[256,256]{1,0:T(8,128)(2,1)}, u32[]{:S(2)}) copy-start(bf16[256,256]{1,0:T(8,128)(2,1)} %refs_1_.4) | copy-start | bytes 393220
  19.5 31.2 %copy-start.7 = (bf16[256,256]{1,0:T(8,128)(2,1)S(1)}, bf16[256,256]{1,0:T(8,128)(2,1)}, u32[]{:S(2)}) copy-start(bf16[256,256]{1,0:T(8,128)(2,1)} %refs_2_.4) | copy-start | bytes 393220
  19.6 31.2 %copy-start.8 = (f32[256]{0:T(256)S(1)}, f32[256]{0:T(256)}, u32[]{:S(2)}) copy-start(f32[256]{0:T(256)} %param.17) | copy-start | bytes 3076
  20.3 50.4 %copy-start = (bf16[512,384]{1,0:T(8,128)(2,1)S(1)}, bf16[512,384]{1,0:T(8,128)(2,1)}, u32[]{:S(2)}) copy-start(bf16[512,384]{1,0:T(8,128)(2,1)} %constant.17.clone.refs_1_) | copy-start | bytes 1179652
  70.7 14.5 %copy-start.4 = (bf16[512,384]{1,0:T(8,128)(2,1)S(1)}, bf16[512,384]{1,0:T(8,128)(2,1)}, u32[]{:S(2)}) copy-start(bf16[512,384]{1,0:T(8,128)(2,1)} %constant.15.clone.refs_1_) | copy-start | bytes 1179652

commit v7 on v6

--- a/solution.py
+++ b/solution.py
@@ -21,7 +21,7 @@
 WAVES = KEEP // G
 LINE = G * PER
 LANES = 128
-ORDER = {"row": [(23 + i) % G for i in range(G)], "col": [(20 + i) % G for i in range(G)]}
+ORDER = {"row": [(21 + i) % G for i in range(G)], "col": [(20 + i) % G for i in range(G)]}
 BF = jnp.bfloat16
 F32 = jnp.float32
 

time: 86.7 us -> 86.7 us (level)
  no operation moved by 1% of the time
where the time goes in v7:
time: 86.7 us; the launch traced here: 86.4 us
  blocking collectives  81.3 us (94%)
  Pallas kernels  4.37 us (5%)
    all_to_all x4, blocking collectives, exchange(): lax.all_to_all(x, axis, split_axis=0, concat_axis=0, tiled=True, axis_ind...  81.3 us
    pallas_call x5, Pallas kernels, call(): pl.pallas_call(kernel, out_shape=shapes, in_specs=[vmem] * len(args), out...  4.37 us

profile of v7, /device:TPU:1, one launch (start us, length us, event | category | flops | bytes accessed | tf_op | source)
XLA Modules:
  0.0 86.4 jit_solution(16947266311762340360)
XLA Ops:
  0.6 0.0 copy-start.1
  0.6 1.4 %s1_.1 = bf16[32,5,4,128]{3,2,1,0:T(4,128)(2,1)S(1)} custom-call(bf16[96,384]{1,0:T(8,128)(2,1)} %bitcast.6, bf16[96,384]{1,0:T(8,128)(2,1)} %bitcast.7, bf16[512,384]{1,0:T(8,128)(2,1)} %constant.14.clone.refs_2_), custom_call_target="tpu_custom_call" | custom-call | tf_op jit(solution)/shard_map/s1/pallas_call | solution.py:203
  2.1 0.0 copy-start.2
  2.1 0.0 copy-start.3
  2.1 0.0 copy-start.5
  2.1 17.4 %all_to_all.20.refs_0_ = bf16[32,5,4,128]{3,2,1,0:T(4,128)(2,1)S(1)} all-to-all(bf16[32,5,4,128]{3,2,1,0:T(4,128)(2,1)S(1)} %s1_.1), channel_id=1, replica_groups={{20,21,22,23,24,25,26,27,28,29,30,31,0,1,2,3,4,5,6,7,8,9,10,11,12,13,14..., dimensions={0} | all-to-all | bytes 327680 | tf_op jit(solution)/shard_map/all_to_all | solution.py:232
  19.5 0.0 copy-done.1
  19.5 0.0 copy-done.2
  19.5 0.0 copy-done.3
  19.5 0.0 copy-done.5
  19.5 0.0 copy-start.6
  19.5 0.0 copy-start.7
  19.6 0.0 copy-start.8
  19.6 0.7 s2_.1
  20.3 0.0 copy-start
  20.3 30.4 %all_to_all.21.refs_0_ = bf16[32,4,384]{2,1,0:T(4,128)(2,1)S(1)} all-to-all(bf16[32,4,384]{2,1,0:T(4,128)(2,1)S(1)} %s2_.1), channel_id=1, replica_groups={{672,704,736,768,800,832,864,896,928,960,992,0,32,64,96,128,160,192,224..., dimensions={0} | all-to-all | bytes 196608 | tf_op jit(solution)/shard_map/all_to_all | solution.py:232
  50.8 0.0 copy-done.6
  50.8 0.0 copy-done.7
  50.8 0.0 copy-done.8
  50.8 0.5 s3.1
  51.3 20.1 %all_to_all.22.refs_0_ = bf16[32,4,384]{2,1,0:T(4,128)(2,1)S(1)} all-to-all(bf16[32,4,384]{2,1,0:T(4,128)(2,1)S(1)} %s3.1), channel_id=1, replica_groups={{672,704,736,768,800,832,864,896,928,960,992,0,32,64,96,128,160,192,224..., dimensions={0} | all-to-all | bytes 196608 | tf_op jit(solution)/shard_map/all_to_all | solution.py:232
  71.4 0.0 copy-done
  71.4 0.0 copy-start.4
  71.4 0.6 s4_.1
  72.0 13.3 %all_to_all.23.refs_0_ = bf16[32,5,4,128]{3,2,1,0:T(4,128)(2,1)S(1)} all-to-all(bf16[32,5,4,128]{3,2,1,0:T(4,128)(2,1)S(1)} %s4_.1), channel_id=1, replica_groups={{20,21,22,23,24,25,26,27,28,29,30,31,0,1,2,3,4,5,6,7,8,9,10,11,12,13,14..., dimensions={0} | all-to-all | bytes 327680 | tf_op jit(solution)/shard_map/all_to_all | solution.py:232
  85.3 0.0 copy-done.4
  85.3 1.1 %s5.1 = (bf16[96,384]{1,0:T(8,128)(2,1)}, bf16[96,384]{1,0:T(8,128)(2,1)}) custom-call(bf16[32,5,4,128]{3,2,1,0:T(4,128)(2,1)S(1)} %all_to_all.23.refs_0_, bf16[512,384]{1,0:T(8,128)(2,1)S(1)} %copy-done.4), custom_call_target="tpu_custom_call" | custom-call | tf_op jit(solution)/shard_map/s5/pallas_call | solution.py:203
Async XLA Ops:
  0.6 18.9 %copy-start.1 = (bf16[384,512]{1,0:T(8,128)(2,1)S(1)}, bf16[384,512]{1,0:T(8,128)(2,1)}, u32[]{:S(2)}) copy-start(bf16[384,512]{1,0:T(8,128)(2,1)} %constant.16.clone.refs_1_) | copy-start | bytes 1179652
  2.1 17.4 %copy-start.2 = (f32[192,128]{1,0:T(8,128)S(1)}, f32[192,128]{1,0:T(8,128)}, u32[]{:S(2)}) copy-start(f32[192,128]{1,0:T(8,128)} %constant.20.clone.refs_4_) | copy-start | bytes 294916
  2.1 17.4 %copy-start.3 = (f32[192,128]{1,0:T(8,128)S(1)}, f32[192,128]{1,0:T(8,128)}, u32[]{:S(2)}) copy-start(f32[192,128]{1,0:T(8,128)} %constant.19.clone.refs_3_) | copy-start | bytes 294916
  2.1 17.4 %copy-start.5 = (bf16[128,256]{1,0:T(8,128)(2,1)S(1)}, bf16[128,256]{1,0:T(8,128)(2,1)}, u32[]{:S(2)}) copy-start(bf16[128,256]{1,0:T(8,128)(2,1)} %constant.18.clone.refs_2_) | copy-start | bytes 196612
  19.5 31.2 %copy-start.6 = (bf16[256,256]{1,0:T(8,128)(2,1)S(1)}, bf16[256,256]{1,0:T(8,128)(2,1)}, u32[]{:S(2)}) copy-start(bf16[256,256]{1,0:T(8,128)(2,1)} %refs_1_.4) | copy-start | bytes 393220
  19.5 31.2 %copy-start.7 = (bf16[256,256]{1,0:T(8,128)(2,1)S(1)}, bf16[256,256]{1,0:T(8,128)(2,1)}, u32[]{:S(2)}) copy-start(bf16[256,256]{1,0:T(8,128)(2,1)} %refs_2_.4) | copy-start | bytes 393220
  19.6 31.2 %copy-start.8 = (f32[256]{0:T(256)S(1)}, f32[256]{0:T(256)}, u32[]{:S(2)}) copy-start(f32[256]{0:T(256)} %param.17) | copy-start | bytes 3076
  20.3 51.1 %copy-start = (bf16[512,384]{1,0:T(8,128)(2,1)S(1)}, bf16[512,384]{1,0:T(8,128)(2,1)}, u32[]{:S(2)}) copy-start(bf16[512,384]{1,0:T(8,128)(2,1)} %constant.17.clone.refs_1_) | copy-start | bytes 1179652
  71.4 13.9 %copy-start.4 = (bf16[512,384]{1,0:T(8,128)(2,1)S(1)}, bf16[512,384]{1,0:T(8,128)(2,1)}, u32[]{:S(2)}) copy-start(bf16[512,384]{1,0:T(8,128)(2,1)} %constant.15.clone.refs_1_) | copy-start | bytes 1179652

commit v8 on v7

--- a/solution.py
+++ b/solution.py
@@ -113,8 +113,8 @@
     first = jnp.where(lane < 96, g[:n, :LANES], one).reshape(G, 2, 4, LANES)
     mid = jnp.where(lane < 96, mid, two).reshape(G, 2, 4, LANES)
     lane = lax.broadcasted_iota(jnp.int32, (G, 4, LANES), 2)
-    low, high = two.reshape(G, 8, LANES)[:, :4], one.reshape(G, 8, LANES)[:, 4:]
-    rest = jnp.where(lane < 32, low, high).reshape(G, 1, 4, LANES)
+    low, high = g[:n, LANES:].reshape(G, 8, LANES)[:, :4], two.reshape(G, 8, LANES)[:, 4:]
+    rest = jnp.where(lane < 64, high, low).reshape(G, 1, 4, LANES)
     return send(jnp.concatenate((first, mid, rest), axis=1), "col").astype(BF)
 
 
@@ -122,10 +122,11 @@
     n = G * 8
     x = receive(x.astype(F32), "col")
     first, mid = x[:, :2].reshape(n, LANES), x[:, 2:4].reshape(n, LANES)
-    rest = jnp.concatenate((x[:, 4], roll(x[:, 4], 96, 2)), axis=1).reshape(n, LANES)
+    rest = jnp.concatenate((x[:, 4], x[:, 4]), axis=1).reshape(n, LANES)
     lane = lax.broadcasted_iota(jnp.int32, (n, LANES), 1)
+    low = lax.broadcasted_iota(jnp.int32, (n, LANES), 0) % 8 < 4
     last = roll(jnp.where(lane < 32, rest, mid), 64, 1)
-    last = jnp.where(lane < 32, roll(first, 32, 1), last)
+    last = jnp.where(lane < 32, roll(first, 32, 1), jnp.where((lane >= 64) & low, rest, last))
     return (
         jnp.concatenate((first, mid), axis=0).astype(BF),
         jnp.concatenate((last, roll(mid, n - 4, 0)), axis=0).astype(BF),

time: 86.7 us -> 86.6 us (level)
  no operation moved by 1% of the time
where the time goes in v8:
time: 86.6 us; the launch traced here: 86.3 us
  blocking collectives  81.3 us (94%)
  Pallas kernels  4.28 us (5%)
    all_to_all x4, blocking collectives, exchange(): lax.all_to_all(x, axis, split_axis=0, concat_axis=0, tiled=True, axis_ind...  81.3 us
    pallas_call x5, Pallas kernels, call(): pl.pallas_call(kernel, out_shape=shapes, in_specs=[vmem] * len(args), out...  4.28 us

profile of v8, /device:TPU:1, one launch (start us, length us, event | category | flops | bytes accessed | tf_op | source)
XLA Modules:
  0.0 86.3 jit_solution(17556326919290384362)
XLA Ops:
  0.6 0.0 copy-start.1
  0.6 1.5 %s1_.1 = bf16[32,5,4,128]{3,2,1,0:T(4,128)(2,1)S(1)} custom-call(bf16[96,384]{1,0:T(8,128)(2,1)} %bitcast.6, bf16[96,384]{1,0:T(8,128)(2,1)} %bitcast.7, bf16[512,384]{1,0:T(8,128)(2,1)} %constant.14.clone.refs_2_), custom_call_target="tpu_custom_call" | custom-call | tf_op jit(solution)/shard_map/s1/pallas_call | solution.py:204
  2.1 0.0 copy-start.2
  2.1 0.0 copy-start.3
  2.1 0.0 copy-start.5
  2.1 17.4 %all_to_all.20.refs_0_ = bf16[32,5,4,128]{3,2,1,0:T(4,128)(2,1)S(1)} all-to-all(bf16[32,5,4,128]{3,2,1,0:T(4,128)(2,1)S(1)} %s1_.1), channel_id=1, replica_groups={{20,21,22,23,24,25,26,27,28,29,30,31,0,1,2,3,4,5,6,7,8,9,10,11,12,13,14..., dimensions={0} | all-to-all | bytes 327680 | tf_op jit(solution)/shard_map/all_to_all | solution.py:233
  19.5 0.0 copy-done.1
  19.5 0.0 copy-done.2
  19.5 0.0 copy-done.3
  19.5 0.0 copy-done.5
  19.5 0.0 copy-start.6
  19.5 0.0 copy-start.7
  19.6 0.0 copy-start.8
  19.6 0.7 s2_.1
  20.3 0.0 copy-start
  20.3 30.4 %all_to_all.21.refs_0_ = bf16[32,4,384]{2,1,0:T(4,128)(2,1)S(1)} all-to-all(bf16[32,4,384]{2,1,0:T(4,128)(2,1)S(1)} %s2_.1), channel_id=1, replica_groups={{672,704,736,768,800,832,864,896,928,960,992,0,32,64,96,128,160,192,224..., dimensions={0} | all-to-all | bytes 196608 | tf_op jit(solution)/shard_map/all_to_all | solution.py:233
  50.7 0.0 copy-done.6
  50.7 0.0 copy-done.7
  50.7 0.0 copy-done.8
  50.7 0.5 s3.1
  51.3 20.1 %all_to_all.22.refs_0_ = bf16[32,4,384]{2,1,0:T(4,128)(2,1)S(1)} all-to-all(bf16[32,4,384]{2,1,0:T(4,128)(2,1)S(1)} %s3.1), channel_id=1, replica_groups={{672,704,736,768,800,832,864,896,928,960,992,0,32,64,96,128,160,192,224..., dimensions={0} | all-to-all | bytes 196608 | tf_op jit(solution)/shard_map/all_to_all | solution.py:233
  71.4 0.0 copy-done
  71.4 0.0 copy-start.4
  71.4 0.6 s4_.1
  72.0 13.3 %all_to_all.23.refs_0_ = bf16[32,5,4,128]{3,2,1,0:T(4,128)(2,1)S(1)} all-to-all(bf16[32,5,4,128]{3,2,1,0:T(4,128)(2,1)S(1)} %s4_.1), channel_id=1, replica_groups={{20,21,22,23,24,25,26,27,28,29,30,31,0,1,2,3,4,5,6,7,8,9,10,11,12,13,14..., dimensions={0} | all-to-all | bytes 327680 | tf_op jit(solution)/shard_map/all_to_all | solution.py:233
  85.3 0.0 copy-done.4
  85.3 1.0 %s5.1 = (bf16[96,384]{1,0:T(8,128)(2,1)}, bf16[96,384]{1,0:T(8,128)(2,1)}) custom-call(bf16[32,5,4,128]{3,2,1,0:T(4,128)(2,1)S(1)} %all_to_all.23.refs_0_, bf16[512,384]{1,0:T(8,128)(2,1)S(1)} %copy-done.4), custom_call_target="tpu_custom_call" | custom-call | tf_op jit(solution)/shard_map/s5/pallas_call | solution.py:204
Async XLA Ops:
  0.6 18.9 %copy-start.1 = (bf16[384,512]{1,0:T(8,128)(2,1)S(1)}, bf16[384,512]{1,0:T(8,128)(2,1)}, u32[]{:S(2)}) copy-start(bf16[384,512]{1,0:T(8,128)(2,1)} %constant.16.clone.refs_1_) | copy-start | bytes 1179652
  2.1 17.4 %copy-start.2 = (f32[192,128]{1,0:T(8,128)S(1)}, f32[192,128]{1,0:T(8,128)}, u32[]{:S(2)}) copy-start(f32[192,128]{1,0:T(8,128)} %constant.20.clone.refs_4_) | copy-start | bytes 294916
  2.1 17.4 %copy-start.3 = (f32[192,128]{1,0:T(8,128)S(1)}, f32[192,128]{1,0:T(8,128)}, u32[]{:S(2)}) copy-start(f32[192,128]{1,0:T(8,128)} %constant.19.clone.refs_3_) | copy-start | bytes 294916
  2.1 17.4 %copy-start.5 = (bf16[128,256]{1,0:T(8,128)(2,1)S(1)}, bf16[128,256]{1,0:T(8,128)(2,1)}, u32[]{:S(2)}) copy-start(bf16[128,256]{1,0:T(8,128)(2,1)} %constant.18.clone.refs_2_) | copy-start | bytes 196612
  19.5 31.2 %copy-start.6 = (bf16[256,256]{1,0:T(8,128)(2,1)S(1)}, bf16[256,256]{1,0:T(8,128)(2,1)}, u32[]{:S(2)}) copy-start(bf16[256,256]{1,0:T(8,128)(2,1)} %refs_1_.4) | copy-start | bytes 393220
  19.5 31.2 %copy-start.7 = (bf16[256,256]{1,0:T(8,128)(2,1)S(1)}, bf16[256,256]{1,0:T(8,128)(2,1)}, u32[]{:S(2)}) copy-start(bf16[256,256]{1,0:T(8,128)(2,1)} %refs_2_.4) | copy-start | bytes 393220
  19.6 31.2 %copy-start.8 = (f32[256]{0:T(256)S(1)}, f32[256]{0:T(256)}, u32[]{:S(2)}) copy-start(f32[256]{0:T(256)} %param.17) | copy-start | bytes 3076
  20.3 51.1 %copy-start = (bf16[512,384]{1,0:T(8,128)(2,1)S(1)}, bf16[512,384]{1,0:T(8,128)(2,1)}, u32[]{:S(2)}) copy-start(bf16[512,384]{1,0:T(8,128)(2,1)} %constant.17.clone.refs_1_) | copy-start | bytes 1179652
  71.4 13.9 %copy-start.4 = (bf16[512,384]{1,0:T(8,128)(2,1)S(1)}, bf16[512,384]{1,0:T(8,128)(2,1)}, u32[]{:S(2)}) copy-start(bf16[512,384]{1,0:T(8,128)(2,1)} %constant.15.clone.refs_1_) | copy-start | bytes 1179652

commit v9 on v8

--- a/solution.py
+++ b/solution.py
@@ -167,7 +167,9 @@
 
 def stage3(x, forward_y, back_y, wall, row_at, col_at):
     c = dot(forward_y, unfold(x))
-    total = jnp.broadcast_to(wall, (LINE, NY)).T + wave_numbers(row_at, col_at)
+    wall = jnp.broadcast_to(wall, (LANES, NY)).T
+    wall = jnp.concatenate((wall, wall[:, : LINE - LANES]), axis=1)
+    total = wall + wave_numbers(row_at, col_at)
     hat = c / jnp.where(row_at < G // 2, -total, 1.0 + DIFFUSION * total)
     return fold(dot(back_y, hat.astype(BF)))
 

time: 86.6 us -> 86.6 us (level)
  no operation moved by 1% of the time
where the time goes in v9:
time: 86.6 us; the launch traced here: 86.3 us
  blocking collectives  81.3 us (94%)
  Pallas kernels  4.28 us (5%)
    all_to_all x4, blocking collectives, exchange(): lax.all_to_all(x, axis, split_axis=0, concat_axis=0, tiled=True, axis_ind...  81.3 us
    pallas_call x5, Pallas kernels, call(): pl.pallas_call(kernel, out_shape=shapes, in_specs=[vmem] * len(args), out...  4.28 us

profile of v9, /device:TPU:1, one launch (start us, length us, event | category | flops | bytes accessed | tf_op | source)
XLA Modules:
  0.0 86.3 jit_solution(14692775934513109753)
XLA Ops:
  0.6 0.0 copy-start.1
  0.6 1.5 %s1_.1 = bf16[32,5,4,128]{3,2,1,0:T(4,128)(2,1)S(1)} custom-call(bf16[96,384]{1,0:T(8,128)(2,1)} %bitcast.6, bf16[96,384]{1,0:T(8,128)(2,1)} %bitcast.7, bf16[512,384]{1,0:T(8,128)(2,1)} %constant.14.clone.refs_2_), custom_call_target="tpu_custom_call" | custom-call | tf_op jit(solution)/shard_map/s1/pallas_call | solution.py:206
  2.1 0.0 copy-start.2
  2.1 0.0 copy-start.3
  2.1 0.0 copy-start.5
  2.1 17.4 %all_to_all.20.refs_0_ = bf16[32,5,4,128]{3,2,1,0:T(4,128)(2,1)S(1)} all-to-all(bf16[32,5,4,128]{3,2,1,0:T(4,128)(2,1)S(1)} %s1_.1), channel_id=1, replica_groups={{20,21,22,23,24,25,26,27,28,29,30,31,0,1,2,3,4,5,6,7,8,9,10,11,12,13,14..., dimensions={0} | all-to-all | bytes 327680 | tf_op jit(solution)/shard_map/all_to_all | solution.py:235
  19.5 0.0 copy-done.1
  19.5 0.0 copy-done.2
  19.5 0.0 copy-done.3
  19.5 0.0 copy-done.5
  19.5 0.0 copy-start.6
  19.5 0.0 copy-start.7
  19.6 0.0 copy-start.8
  19.6 0.7 s2_.1
  20.3 0.0 copy-start
  20.3 30.4 %all_to_all.21.refs_0_ = bf16[32,4,384]{2,1,0:T(4,128)(2,1)S(1)} all-to-all(bf16[32,4,384]{2,1,0:T(4,128)(2,1)S(1)} %s2_.1), channel_id=1, replica_groups={{672,704,736,768,800,832,864,896,928,960,992,0,32,64,96,128,160,192,224..., dimensions={0} | all-to-all | bytes 196608 | tf_op jit(solution)/shard_map/all_to_all | solution.py:235
  50.7 0.0 copy-done.6
  50.7 0.0 copy-done.7
  50.7 0.0 copy-done.8
  50.7 0.5 s3.1
  51.3 20.1 %all_to_all.22.refs_0_ = bf16[32,4,384]{2,1,0:T(4,128)(2,1)S(1)} all-to-all(bf16[32,4,384]{2,1,0:T(4,128)(2,1)S(1)} %s3.1), channel_id=1, replica_groups={{672,704,736,768,800,832,864,896,928,960,992,0,32,64,96,128,160,192,224..., dimensions={0} | all-to-all | bytes 196608 | tf_op jit(solution)/shard_map/all_to_all | solution.py:235
  71.4 0.0 copy-done
  71.4 0.0 copy-start.4
  71.4 0.6 s4_.1
  72.0 13.3 %all_to_all.23.refs_0_ = bf16[32,5,4,128]{3,2,1,0:T(4,128)(2,1)S(1)} all-to-all(bf16[32,5,4,128]{3,2,1,0:T(4,128)(2,1)S(1)} %s4_.1), channel_id=1, replica_groups={{20,21,22,23,24,25,26,27,28,29,30,31,0,1,2,3,4,5,6,7,8,9,10,11,12,13,14..., dimensions={0} | all-to-all | bytes 327680 | tf_op jit(solution)/shard_map/all_to_all | solution.py:235
  85.3 0.0 copy-done.4
  85.3 1.0 %s5.1 = (bf16[96,384]{1,0:T(8,128)(2,1)}, bf16[96,384]{1,0:T(8,128)(2,1)}) custom-call(bf16[32,5,4,128]{3,2,1,0:T(4,128)(2,1)S(1)} %all_to_all.23.refs_0_, bf16[512,384]{1,0:T(8,128)(2,1)S(1)} %copy-done.4), custom_call_target="tpu_custom_call" | custom-call | tf_op jit(solution)/shard_map/s5/pallas_call | solution.py:206
Async XLA Ops:
  0.6 18.9 %copy-start.1 = (bf16[384,512]{1,0:T(8,128)(2,1)S(1)}, bf16[384,512]{1,0:T(8,128)(2,1)}, u32[]{:S(2)}) copy-start(bf16[384,512]{1,0:T(8,128)(2,1)} %constant.16.clone.refs_1_) | copy-start | bytes 1179652
  2.1 17.4 %copy-start.2 = (f32[192,128]{1,0:T(8,128)S(1)}, f32[192,128]{1,0:T(8,128)}, u32[]{:S(2)}) copy-start(f32[192,128]{1,0:T(8,128)} %constant.20.clone.refs_4_) | copy-start | bytes 294916
  2.1 17.4 %copy-start.3 = (f32[192,128]{1,0:T(8,128)S(1)}, f32[192,128]{1,0:T(8,128)}, u32[]{:S(2)}) copy-start(f32[192,128]{1,0:T(8,128)} %constant.19.clone.refs_3_) | copy-start | bytes 294916
  2.1 17.4 %copy-start.5 = (bf16[128,256]{1,0:T(8,128)(2,1)S(1)}, bf16[128,256]{1,0:T(8,128)(2,1)}, u32[]{:S(2)}) copy-start(bf16[128,256]{1,0:T(8,128)(2,1)} %constant.18.clone.refs_2_) | copy-start | bytes 196612
  19.5 31.2 %copy-start.6 = (bf16[256,256]{1,0:T(8,128)(2,1)S(1)}, bf16[256,256]{1,0:T(8,128)(2,1)}, u32[]{:S(2)}) copy-start(bf16[256,256]{1,0:T(8,128)(2,1)} %refs_1_.4) | copy-start | bytes 393220
  19.5 31.2 %copy-start.7 = (bf16[256,256]{1,0:T(8,128)(2,1)S(1)}, bf16[256,256]{1,0:T(8,128)(2,1)}, u32[]{:S(2)}) copy-start(bf16[256,256]{1,0:T(8,128)(2,1)} %refs_2_.4) | copy-start | bytes 393220
  19.6 31.2 %copy-start.8 = (f32[256]{0:T(256)S(1)}, f32[256]{0:T(256)}, u32[]{:S(2)}) copy-start(f32[256]{0:T(256)} %param.17) | copy-start | bytes 3076
  20.3 51.1 %copy-start = (bf16[512,384]{1,0:T(8,128)(2,1)S(1)}, bf16[512,384]{1,0:T(8,128)(2,1)}, u32[]{:S(2)}) copy-start(bf16[512,384]{1,0:T(8,128)(2,1)} %constant.17.clone.refs_1_) | copy-start | bytes 1179652
  71.4 13.9 %copy-start.4 = (bf16[512,384]{1,0:T(8,128)(2,1)S(1)}, bf16[512,384]{1,0:T(8,128)(2,1)}, u32[]{:S(2)}) copy-start(bf16[512,384]{1,0:T(8,128)(2,1)} %constant.15.clone.refs_1_) | copy-start | bytes 1179652
